TPU v7x, 128 devices: a whole 4x4x4 slice. The times are simulated.
128 devices in a mesh: shard: 32 (over y, x, core), tp: 4 (over z).
Axes of the slice: x: 4, y: 4, z: 4, core: 2. Of those that a mesh axis runs over, the one named last changes fastest.
Arguments:
- weight_gate: bfloat16 [2560, 9728], P('shard', 'tp'), may hold values from -0.21875 to 0.21875
- low_gate: bfloat16 [2560, 32], P('shard'), may hold values from -0.125 to 0.125
- high_gate: bfloat16 [32, 9728], P(None, 'tp'), may hold values from -1 to 1
- weight_up: bfloat16 [2560, 9728], P('shard', 'tp'), may hold values from -0.21875 to 0.21875
- low_up: bfloat16 [2560, 32], P('shard'), may hold values from -0.125 to 0.125
- high_up: bfloat16 [32, 9728], P(None, 'tp'), may hold values from -1 to 1
- norm_gain: float32 [2560], P('shard'), may hold values from 0.25 to 1.75
Outputs:
- ready_gate: bfloat16 [2560, 9728], P(None, 'tp')
- ready_up: bfloat16 [2560, 9728], P(None, 'tp')
- factor_gate: float32 [9728], P('tp')
- factor_up: float32 [9728], P('tp')
All inputs are finite; a program needn't handle non-finite values.
Results may differ from a plain program's by a relative error of at most 0.001.
Values may be sent and summed in bfloat16 or wider, within the bound.
No kernel may reach another device: no remote copies, remote signals or barrier semaphores. Data moves between devices by JAX's collectives and lax.ppermute only.
A program may use at most 128 MiB of HBM per device.

v0:
```python
import jax
import jax.numpy as jnp
from jax import lax
from jax.sharding import PartitionSpec as P

mix_rate = 2.0


def sent_to_all(array, axis):
    size = lax.axis_size(axis)
    return lax.all_to_all(
        jnp.broadcast_to(array[None], (size, *array.shape)), axis, 0, 0, tiled=True
    )


def taken_together(array, axis):
    everything = sent_to_all(array, axis)
    return jnp.sum(everything, axis=0)


def in_one(arrays, axis):
    ends = [0]
    for a in arrays:
        ends.append(ends[-1] + a.size)
    so_far = taken_together(jnp.concatenate([a.ravel() for a in arrays]), axis)
    return tuple((so_far[b:e].reshape(a.shape) for a, b, e in zip(arrays, ends, ends[1:])))


def in_one_piece(arrays, axis, dim, along):
    widths = [a.shape[along] for a in arrays]
    both = jnp.concatenate(arrays, axis=along)
    filled = lax.all_gather(both, axis, axis=dim, tiled=True)
    return tuple(jnp.split(filled, [sum(widths[:k]) for k in range(1, len(widths))], axis=along))


def local(weight_gate, low_gate, high_gate, weight_up, low_up, high_up, norm_gain):
    latest_gate = weight_gate.astype(jnp.float32) + mix_rate * jnp.dot(
        low_gate, high_gate, preferred_element_type=jnp.float32
    )
    latest_up = weight_up.astype(jnp.float32) + mix_rate * jnp.dot(
        low_up, high_up, preferred_element_type=jnp.float32
    )
    latest_gained_gate = latest_gate * norm_gain[:, None]
    latest_gained_up = latest_up * norm_gain[:, None]
    total_gate, total_up = in_one(
        (
            jnp.sum(latest_gained_gate * latest_gained_gate, axis=0),
            jnp.sum(latest_gained_up * latest_gained_up, axis=0),
        ),
        "shard",
    )
    factor_gate = jnp.sqrt(total_gate)
    factor_up = jnp.sqrt(total_up)
    narrow_gate, narrow_up = (
        (latest_gained_gate / factor_gate).astype(jnp.bfloat16),
        (latest_gained_up / factor_up).astype(jnp.bfloat16),
    )
    ready_gate, ready_up = in_one_piece((narrow_gate, narrow_up), "shard", 0, 1)
    return (ready_gate, ready_up, factor_gate, factor_up)


def solution(mesh):
    in_specs = (
        P("shard", "tp"),
        P("shard", None),
        P(None, "tp"),
        P("shard", "tp"),
        P("shard", None),
        P(None, "tp"),
        P("shard"),
    )
    out_specs = (P(None, "tp"), P(None, "tp"), P("tp"), P("tp"))
    return jax.shard_map(local, mesh=mesh, in_specs=in_specs, out_specs=out_specs, check_vma=False)
```

profile of v0, /device:TPU:1, one launch (start us, length us, event | category | flops | bytes accessed | tf_op | source)
XLA Modules:
  0.0 147.7 jit_solution(14768416146276575479)
XLA Ops:
  7.2 0.0 copy-start
  7.2 0.0 all-gather.2.cloned.1.call-start
  7.2 0.9 copy-done
  8.1 1.4 multiply_reduce_fusion.1
  9.5 1.5 multiply_reduce_fusion
  11.0 0.3 broadcast_in_dim.2
  11.3 20.8 %all_to_all.6 = f32[32,1,4864]{2,1,0:T(1,128)S(1)} all-to-all(f32[32,1,4864]{2,1,0:T(1,128)S(1)} %broadcast_in_dim.2), channel_id=1, replica_groups=mesh['shard'=32,'tp'=4] {'shard'}, dimensions={0} | all-to-all | bytes 1245184 | tf_op jit(solution)/shard_map/all_to_all | solution.py:11
  32.1 0.4 reduce_sum.29
  32.5 0.0 copy-start.1
  32.5 0.0 copy-start.2
  32.5 0.1 divide_convert_fusion
  32.7 0.9 pad_maximum_fusion
  33.6 0.0 all-gather.2.cloned.1.call-update
  33.6 90.2 %all-gather.2.cloned.1.call-done = bf16[2560,4864]{1,0:T(8,128)(2,1)} async-done(((bf16[80,4864]{1,0:T(8,128)(2,1)}), bf16[2560,4864]{1,0:T(8,128)(2,1)}) %all-gather.2.cloned.1.call-update) | async-done | bytes 24903696 | tf_op jit(solution)/shard_map/all_gather | solution.py:32
  123.8 17.0 %fusion.4 = (bf16[2560,2432]{1,0:T(8,128)(2,1)}, bf16[2560,2432]{1,0:T(8,128)(2,1)}) fusion(bf16[2560,4864]{1,0:T(8,128)(2,1)} %all-gather.2.cloned.1.call-done), kind=kLoop, calls=%fused_computation.14 | loop fusion | bytes 49807360 | tf_op jit(solution)/shard_map/split | solution.py:33
  140.8 0.0 copy-done.1
  140.8 0.0 copy-done.2
  (2 shorter events, 0.0 us)
Async XLA Ops:
  7.2 0.9 copy-start
  7.2 116.6 %all-gather.2.cloned.1.call-start = ((), (), s32[]{:S(2)}) async-start(), calls=%async_computation.1 | async-start | bytes 25681920 | tf_op jit(solution)/shard_map/all_gather | solution.py:32
  32.5 108.3 %copy-start.1 = (f32[2432]{0:T(1024)}, f32[2432]{0:T(1024)S(1)}, u32[]{:S(2)}) copy-start(f32[2432]{0:T(1024)S(1)} %get-tuple-element.6) | copy-start | bytes 29188
  32.5 108.3 %copy-start.2 = (f32[2432]{0:T(1024)}, f32[2432]{0:T(1024)S(1)}, u32[]{:S(2)}) copy-start(f32[2432]{0:T(1024)S(1)} %get-tuple-element.7) | copy-start | bytes 29188
Sparse Core Ops, SparseCore 0:
  33.8 89.9 all-gather.1
where the time goes:
time: 148 us
  waiting for transfers between devices  90.2 us (61%)
  blocking collectives  20.8 us (14%)
  local copies, waits for them, and re-layouts  18.2 us (12%)
  between operations  14.1 us (10%)
  matrix products  2.84 us (2%)
    all_gather x1, waiting for transfers between devices, in_one_piece(): filled = lax.all_gather(both, axis, axis=dim, tiled=True)  90.2 us
    all_to_all x1, blocking collectives, sent_to_all(): lax.all_to_all(jnp.broadcast_to(array[None], (size, *array.shape)), axis,...  20.8 us
    split x1, local copies, waits for them, and re-layouts, in_one_piece(): jnp.split(filled, [sum(widths[:k]) for k in range(1, len(widths))], axis=...  17 us
  transfers between devices with their start and end apart: 1, of which 1 were waited for; matrix products, arithmetic and copies ran while one was open for 0% of the time, Pallas kernels for 0%

commit v1 on v0

v1 whole, which is shorter than its diff:
```python
import functools

import jax
import jax.numpy as jnp
from jax import lax
from jax.experimental import pallas as pl
from jax.experimental.pallas import tpu as pltpu
from jax.sharding import PartitionSpec as P


ROWS = 80
HALF = 2432
WIDE = 2 * HALF
FULL = WIDE + 128
TILE = 256
KIB = 1024
RANK = 32
TOP = 48
mix_rate = 2.0


def shard_of(y, x, c):
    return ((y % 4) * 4 + x % 4) * 2 + c


def hops(core0, core1, flip=0):
    step = (core0, core1)
    return [
        (shard_of(y, x, c), shard_of(y + step[c][0], x + step[c][1], c ^ flip))
        for y in range(4)
        for x in range(4)
        for c in range(2)
    ]


FIRST = {1: hops((0, 1), (1, 0)), -1: hops((0, -1), (-1, 0))}
SECOND = {1: hops((1, 0), (0, 1)), -1: hops((-1, 0), (0, -1))}
SIDE = hops((0, 0), (0, 0), 1)
ALONG_X = {d: hops((0, d), (0, d)) for d in (1, -1, 2)}
ALONG_Y = {d: hops((d, 0), (d, 0)) for d in (1, -1, 2)}


def source(first, second, flip):
    me = lax.axis_index("shard")
    core, x, y = (me & 1) ^ flip, (me >> 1) & 3, me >> 3
    sx = (x + jnp.where(core == 0, first, second)) & 3
    sy = (y + jnp.where(core == 0, second, first)) & 3
    return ((sy << 2) + sx) * 2 + core


def sent(array, pairs):
    return lax.ppermute(array, "shard", pairs)


def in_vmem(n):
    return [pl.BlockSpec(memory_space=pltpu.VMEM)] * n


def pack_kernel(gate, up, low_gate_t, low_up_t, gain, high_gate, high_up, block, high, low_v, gain_v, side, sems):
    moves = (
        (low_gate_t, low_v.at[0]),
        (low_up_t, low_v.at[1]),
        (gain, gain_v),
        (gate, block.at[:, pl.ds(0, HALF)]),
        (up, block.at[:, pl.ds(HALF, HALF)]),
        (high_gate, high.at[pl.ds(0, RANK), pl.ds(0, HALF)]),
        (high_up, high.at[pl.ds(RANK, RANK), pl.ds(HALF, HALF)]),
    )
    copies = [pltpu.make_async_copy(src, dst, sems.at[k]) for k, (src, dst) in enumerate(moves)]
    for copy in copies:
        copy.start()
    high[0:RANK, HALF:] = jnp.zeros((RANK, HALF), jnp.bfloat16)
    high[RANK : 2 * RANK, :HALF] = jnp.zeros((RANK, HALF), jnp.bfloat16)
    side[...] = jnp.zeros_like(side)
    for copy in copies[:3]:
        copy.wait()
    g = gain_v[...]
    hi = g.astype(jnp.bfloat16).astype(jnp.float32)
    mid = (g - hi).astype(jnp.bfloat16).astype(jnp.float32)
    side[0:32, 0:ROWS] = low_v[0].astype(jnp.float32) * mix_rate
    side[32:64, 0:ROWS] = low_v[1].astype(jnp.float32) * mix_rate
    side[64:65, 0:ROWS] = hi
    side[65:66, 0:ROWS] = mid
    side[66:67, 0:ROWS] = g - hi - mid
    block[:, WIDE:] = side[...].T[0:ROWS].astype(jnp.bfloat16)
    for copy in copies[3:]:
        copy.wait()


def gain_of(extra):
    row = lax.broadcasted_iota(jnp.int32, (128, 128), 0)
    ones = jnp.where((row >= 64) & (row < 67), 1.0, 0.0).astype(jnp.bfloat16)
    g = jnp.dot(extra, ones, preferred_element_type=jnp.float32)
    return jnp.concatenate([g, g], axis=1)


def sums_kernel(block, high, sums):
    extra = block[:, WIDE:]
    gain = gain_of(extra)
    for j in range(WIDE // TILE):
        cols = pl.ds(j * TILE, TILE)
        v = block[:, cols].astype(jnp.float32) + jnp.dot(
            extra[:, :64], high[:, cols], preferred_element_type=jnp.float32
        )
        v = v * gain
        sums[:, cols] = jnp.sum(v * v, axis=0, keepdims=True)


def add_kernel(a, b, total):
    total[...] = a[...] + b[...]


def ring_kernel(bit, own, plus, minus, far, *outs):
    even = ((lax.axis_index("shard") >> bit) & 1) == 0
    p, m = plus[...], minus[...]
    partner, other = jnp.where(even, m, p), jnp.where(even, p, m)
    total = (own[...] + partner) + (other + far[...])
    if len(outs) == 1:
        outs[0][...] = total
        return
    factor = jnp.sqrt(total)
    outs[0][...] = factor
    outs[1][...] = 1.0 / factor


def halves_kernel(a, b, top, bottom):
    top[...] = a[:TOP]
    bottom[...] = b[TOP:]


def joined_kernel(top, bottom, block):
    block[:TOP] = top[...]
    block[TOP:] = bottom[...]


def merge_kernel(mine, theirs, *refs):
    n, place = len(mine), len(theirs)
    blocks, refs = refs[:n], refs[n:]
    high, inv = refs[0], refs[1]
    moved, refs = refs[2 : 2 + (place > 0)], refs[2 + (place > 0) :]
    out_gate, out_up, ready, sems = refs[2:]
    outs = (out_gate, out_up)
    copies = []

    def send(src, at, flip, h):
        row = pl.multiple_of(source(*at, flip) * ROWS, ROWS)
        copy = pltpu.make_async_copy(
            src.at[:, pl.ds(h * HALF, HALF)],
            outs[h].at[pl.ds(row, ROWS), :],
            sems.at[len(copies)],
        )
        copy.start()
        copies.append(copy)

    for k in range(place):
        for h in range(2):
            send(moved[0].at[k], theirs[k], 1, h)
    extra = jnp.concatenate([b[:, WIDE:] for b in blocks], axis=0)
    gain = gain_of(extra)
    for j in range(WIDE // TILE):
        cols = pl.ds(j * TILE, TILE)
        low_rank = jnp.dot(extra[:, :64], high[:, cols], preferred_element_type=jnp.float32)
        scale = inv[:, cols]
        for k in range(n):
            rows = slice(k * ROWS, (k + 1) * ROWS)
            v = blocks[k][:, cols].astype(jnp.float32) + low_rank[rows]
            ready[k, :, cols] = (v * gain[rows] * scale).astype(jnp.bfloat16)
        if j == HALF // TILE:
            for k in range(n):
                send(ready.at[k], mine[k], 0, 0)
    for k in range(n):
        send(ready.at[k], mine[k], 0, 1)
    for copy in copies:
        copy.wait()


def place_kernel(theirs, *refs):
    moved, refs = refs[: len(theirs)], refs[len(theirs) + 2 :]
    outs, sems = refs[:2], refs[2]
    copies = []
    for i, pair in enumerate(theirs):
        for k, at in enumerate(pair):
            row = pl.multiple_of(source(*at, 1) * ROWS, ROWS)
            for h, out in enumerate(outs):
                copy = pltpu.make_async_copy(
                    moved[i].at[k, :, pl.ds(h * HALF, HALF)],
                    out.at[pl.ds(row, ROWS), :],
                    sems.at[len(copies)],
                )
                copy.start()
                copies.append(copy)
    for copy in copies:
        copy.wait()


OUT = jax.ShapeDtypeStruct((32 * ROWS, HALF), jnp.bfloat16)
ANY = pl.BlockSpec(memory_space=pl.ANY)


def params(mib):
    return pltpu.CompilerParams(vmem_limit_bytes=int(mib * KIB * KIB))


def cost(us):
    return pl.CostEstimate(flops=int(us * 1e3 * 4000), bytes_accessed=1, transcendentals=0)


def small(body, outs, mib, *operands, scratch=(), specs=None):
    return pl.pallas_call(
        body,
        out_shape=outs,
        in_specs=specs or in_vmem(len(operands)),
        out_specs=jax.tree.map(lambda _: pl.BlockSpec(memory_space=pltpu.VMEM), outs),
        scratch_shapes=scratch,
        compiler_params=params(mib),
        cost_estimate=cost(1.0),
    )(*operands)


def merged(blocks, mine, theirs, high, inv, moved, outs):
    operands = [*blocks, high, inv, *moved]
    count = len(operands)
    aliases = {}
    specs = in_vmem(count)
    if outs is None:
        outs = ()

        def body(*refs):
            merge_kernel(mine, theirs, *refs[:count], None, None, *refs[count:])
    else:
        aliases = {count: 0, count + 1: 1}
        specs = specs + [ANY, ANY]
        body = functools.partial(merge_kernel, mine, theirs)
    n = len(mine)
    return pl.pallas_call(
        body,
        out_shape=(OUT, OUT, jax.ShapeDtypeStruct((n, ROWS, WIDE), jnp.bfloat16)),
        in_specs=specs,
        out_specs=(ANY, ANY, pl.BlockSpec(memory_space=pltpu.VMEM)),
        scratch_shapes=[pltpu.SemaphoreType.DMA((2 * (n + len(theirs)),))],
        input_output_aliases=aliases,
        compiler_params=params(14),
        cost_estimate=cost(1.5),
    )(*operands, *outs)


def placed(theirs, moved, outs):
    n = len(moved)
    return pl.pallas_call(
        functools.partial(place_kernel, theirs),
        out_shape=(OUT, OUT),
        in_specs=in_vmem(n) + [ANY, ANY],
        out_specs=(ANY, ANY),
        scratch_shapes=[pltpu.SemaphoreType.DMA((2 * sum(map(len, theirs)),))],
        input_output_aliases={n: 0, n + 1: 1},
        compiler_params=params(10),
        cost_estimate=cost(1.0),
    )(*moved, *outs)


def program(weight_gate, low_gate, high_gate, weight_up, low_up, high_up, norm_gain):
    hbm = pl.BlockSpec(memory_space=pltpu.HBM)
    shape = jax.ShapeDtypeStruct
    a_block = shape((ROWS, FULL), jnp.bfloat16)
    a_sum = shape((1, WIDE), jnp.float32)
    block, high = small(
        pack_kernel,
        (a_block, shape((2 * RANK, WIDE), jnp.bfloat16)),
        62.4,
        weight_gate,
        weight_up,
        low_gate.T,
        low_up.T,
        norm_gain.reshape(1, ROWS),
        high_gate,
        high_up,
        specs=[hbm] * 7,
        scratch=[
            pltpu.VMEM((2, RANK, ROWS), jnp.bfloat16),
            pltpu.VMEM((1, ROWS), jnp.float32),
            pltpu.VMEM((128, 128), jnp.float32),
            pltpu.SemaphoreType.DMA((7,)),
        ],
    )
    held = {(0, 0): block}
    for step in (1, -1):
        held[-step, 0] = sent(block, FIRST[step])
    for step in (1, -1):
        held[0, -step] = sent(block, SECOND[step])

    sums = small(sums_kernel, a_sum, 6, block, high)
    total = small(add_kernel, a_sum, 2, sums, sent(sums, SIDE))
    for axis, along, bit in (("x", ALONG_X, 1), ("y", ALONG_Y, 3)):
        others = [sent(total, along[d]) for d in (1, -1, 2)]
        total = small(
            functools.partial(ring_kernel, bit),
            a_sum if axis == "x" else (a_sum, a_sum),
            2,
            total,
            *others,
        )
    factor, inv = total

    top, bottom = small(
        halves_kernel,
        (shape((TOP, FULL), jnp.bfloat16), shape((ROWS - TOP, FULL), jnp.bfloat16)),
        6,
        held[-1, 0],
        held[1, 0],
    )
    top, bottom = sent(top, FIRST[1]), sent(bottom, FIRST[-1])
    held[2, 0] = small(joined_kernel, a_block, 6, top, bottom)

    for step, order in ((1, (-1, 1, 2)), (-1, (1, -1, 2))):
        for f in order:
            held[f, -step] = sent(held[f, 0], SECOND[step])
    for step, order in ((1, (0, -1)), (-1, (1, 2))):
        for f in order:
            held[f, 2] = sent(held[f, -step], SECOND[step])

    pairs = (
        ((0, 0), (-1, 0)),
        ((0, -1), (0, 1)),
        ((1, 0), (2, 0)),
        ((-1, -1), (1, 1)),
        ((1, -1), (-1, 1)),
        ((2, -1), (2, 1)),
        ((0, 2), (1, 2)),
        ((-1, 2), (2, 2)),
    )
    outs, moved = None, []
    for k, pair in enumerate(pairs):
        late = k - 2
        *outs, ready = merged(
            [held[p] for p in pair],
            pair,
            pairs[late] if late >= 0 else (),
            high,
            inv,
            [moved[late]] if late >= 0 else [],
            outs,
        )
        moved.append(sent(ready, SIDE))
    ready_gate, ready_up = placed(pairs[-2:], moved[-2:], outs)
    factor = factor.reshape(WIDE)
    return ready_gate, ready_up, factor[:HALF], factor[HALF:]


def solution(mesh):
    in_specs = (
        P("shard", "tp"),
        P("shard", None),
        P(None, "tp"),
        P("shard", "tp"),
        P("shard", None),
        P(None, "tp"),
        P("shard"),
    )
    out_specs = (P(None, "tp"), P(None, "tp"), P("tp"), P("tp"))
    return jax.shard_map(program, mesh=mesh, in_specs=in_specs, out_specs=out_specs, check_vma=False)
```

time: 148 us -> 140 us (0.946)
  starting transfers between devices: 0.04 us -> 45.8 us
  waiting for transfers between devices: 90.2 us -> 68.7 us
  blocking collectives: 20.8 us -> 0 us
  Pallas kernels: 0 us -> 20.7 us
  local copies, waits for them, and re-layouts: 18.2 us -> 3.87 us
  between operations: 14.1 us -> 0.95 us
  matrix products: 2.84 us -> 0 us
    all_gather x1 -> x0, waiting for transfers between devices: 90.2 us -> none  [in_one_piece(): filled = lax.all_gather(both, axis, axis=dim, tiled=True)]
    ppermute x0 -> x31, waiting for transfers between devices: none -> 68.7 us  [sent(): return lax.ppermute(array, 'shard', pairs)]
    ppermute x0 -> x31, starting transfers between devices: none -> 45.8 us  [sent(): return lax.ppermute(array, 'shard', pairs)]
    all_to_all x1 -> x0, blocking collectives: 20.8 us -> none  [sent_to_all(): lax.all_to_all(jnp.broadcast_to(array[None], (size, *array.shape)), axis,...]
    pallas_call x0 -> x16, Pallas kernels: none -> 20.7 us  [the longest x8 14.8 us: merged(): pl.pallas_call(body, out_shape=(OUT, OUT, jax.ShapeDtypeStruct((n, ROWS,...]
    split x1 -> x0, local copies, waits for them, and re-layouts: 17 us -> none  [in_one_piece(): jnp.split(filled, [sum(widths[:k]) for k in range(1, len(widths))], axis=...]
    dot_general x2 -> x0, matrix products: 2.84 us -> none  [the longest x1 1.46 us: local(): jnp.dot(low_up, high_up, preferred_element_type=jnp.float32)]
    unnamed x6, local copies, waits for them, and re-layouts: 0.88 us -> 3.22 us
  transfers between devices with their start and end apart: 1 -> 31, of which waited for: 1 -> 16; matrix products, arithmetic and copies ran while one was open for 0% -> 0% of each run, Pallas kernels for 0% -> 11%
where the time goes in v1:
time: 140 us
  waiting for transfers between devices  68.7 us (49%)
  starting transfers between devices  45.8 us (33%)
  Pallas kernels  20.7 us (15%)
  local copies, waits for them, and re-layouts  3.87 us (3%)
    ppermute x31, waiting for transfers between devices, sent(): return lax.ppermute(array, 'shard', pairs)  68.7 us
    ppermute x31, starting transfers between devices, sent(): return lax.ppermute(array, 'shard', pairs)  45.8 us
    pallas_call x8, Pallas kernels, merged(): pl.pallas_call(body, out_shape=(OUT, OUT, jax.ShapeDtypeStruct((n, ROWS,...  14.8 us
    pallas_call x7, Pallas kernels, small(): pl.pallas_call(body, out_shape=outs, in_specs=specs or in_vmem(len(operan...  4.17 us
    unnamed x6, local copies, waits for them, and re-layouts  3.22 us
  transfers between devices with their start and end apart: 31, of which 16 were waited for; matrix products, arithmetic and copies ran while one was open for 0% of the time, Pallas kernels for 11%

profile of v1, /device:TPU:1, one launch (start us, length us, event | category | flops | bytes accessed | tf_op | source)
XLA Modules:
  0.0 140.0 jit_solution(7817639445531964471)
XLA Ops:
  0.6 2.5 %shard_map.102 = (bf16[80,4992]{1,0:T(8,128)(2,1)}, bf16[64,4864]{1,0:T(8,128)(2,1)}) custom-call(bf16[80,2432]{1,0:T(8,128)(2,1)} %gate.1, bf16[80,2432]{1,0:T(8,128)(2,1)} %up.1, bf16[32,80]{1,0:T(8,128)(2,1)} %bitcast.3, bf16[32,80]{1,0:T(8,128)(2,1)} %bitcast.4, f32[1,80]{1,0:T(1,128)} %bitcast.5, bf16[32,2432]{1,0:T(8,128)(2,1)} %high_gate.1, ...), custom_call_target="tpu_custom_call" | custom-call | flops 4000000 | bytes 1 | tf_op jit(solution)/shard_map/pallas_call | solution.py:209
  3.1 2.2 %collective-permute-start.13 = (bf16[80,4992]{1,0:T(8,128)(2,1)}, bf16[80,4992]{1,0:T(8,128)(2,1)S(1)}, u32[]{:S(2)}, u32[]{:S(2)}) collective-permute-start(bf16[80,4992]{1,0:T(8,128)(2,1)} %get-tuple-element.36.block.refs_0_), channel_id=1, source_target_pairs={{0,8},{4,36},{8,16},{12,44},{16,24},{20,52},{24,0},{28,60},{32,40}... | collective-permute-start | bytes 2396168 | tf_op jit(solution)/shard_map/ppermute | solution.py:52
  5.3 1.2 collective-permute-start
  6.5 1.5 %collective-permute-start.18 = (bf16[80,4992]{1,0:T(8,128)(2,1)}, bf16[80,4992]{1,0:T(8,128)(2,1)S(1)}, u32[]{:S(2)}, u32[]{:S(2)}) collective-permute-start(bf16[80,4992]{1,0:T(8,128)(2,1)} %get-tuple-element.36.block.refs_0_), channel_id=1, source_target_pairs={{0,96},{4,28},{8,104},{12,4},{16,112},{20,12},{24,120},{28,20},{32... | collective-permute-start | bytes 2396168 | tf_op jit(solution)/shard_map/ppermute | solution.py:52
  8.0 1.1 copy-done
  9.0 1.6 %shard_map.103.a = f32[1,4864]{1,0:T(1,128)S(1)} custom-call(bf16[80,4992]{1,0:T(8,128)(2,1)} %get-tuple-element.36.block.refs_0_, bf16[64,4864]{1,0:T(8,128)(2,1)S(1)} %copy-done), custom_call_target="tpu_custom_call" | custom-call | flops 4000000 | bytes 1 | tf_op jit(solution)/shard_map/pallas_call | solution.py:209
  10.6 1.5 %collective-permute-start.5 = (f32[1,4864]{1,0:T(1,128)S(1)}, f32[1,4864]{1,0:T(1,128)S(1)}, u32[]{:S(2)}, u32[]{:S(2)}) collective-permute-start(f32[1,4864]{1,0:T(1,128)S(1)} %shard_map.103.a), channel_id=1, source_target_pairs={{0,4},{4,0},{8,12},{12,8},{16,20},{20,16},{24,28},{28,24},{32,36},... | collective-permute-start | bytes 58376 | tf_op jit(solution)/shard_map/ppermute | solution.py:52
  12.1 0.8 collective-permute-done.5.b
  13.0 1.2 collective-permute-start.6
  14.2 1.5 %collective-permute-start.7 = (f32[1,4864]{1,0:T(1,128)S(1)}, f32[1,4864]{1,0:T(1,128)S(1)}, u32[]{:S(2)}, u32[]{:S(2)}) collective-permute-start(f32[1,4864]{1,0:T(1,128)S(1)} %shard_map.104.own), channel_id=1, source_target_pairs={{0,24},{4,28},{8,0},{12,4},{16,8},{20,12},{24,16},{28,20},{32,56},... | collective-permute-start | bytes 58376 | tf_op jit(solution)/shard_map/ppermute | solution.py:52
  15.6 10.7 %collective-permute-done.6.plus = f32[1,4864]{1,0:T(1,128)S(1)} collective-permute-done((f32[1,4864]{1,0:T(1,128)S(1)}, f32[1,4864]{1,0:T(1,128)S(1)}, u32[]{:S(2)}, u32[]{:S(2)}) %collective-permute-start.6) | collective-permute-done | bytes 19488 | tf_op jit(solution)/shard_map/ppermute | solution.py:52
  26.4 1.0 collective-permute-start.2
  27.4 0.0 collective-permute-done.7.minus
  27.4 1.5 %collective-permute-start.8 = (f32[1,4864]{1,0:T(1,128)S(1)}, f32[1,4864]{1,0:T(1,128)S(1)}, u32[]{:S(2)}, u32[]{:S(2)}) collective-permute-start(f32[1,4864]{1,0:T(1,128)S(1)} %shard_map.104.own), channel_id=1, source_target_pairs={{0,16},{4,20},{8,24},{12,28},{16,0},{20,4},{24,8},{28,12},{32,48},... | collective-permute-start | bytes 58376 | tf_op jit(solution)/shard_map/ppermute | solution.py:52
  28.9 2.6 %collective-permute-done.8.far = f32[1,4864]{1,0:T(1,128)S(1)} collective-permute-done((f32[1,4864]{1,0:T(1,128)S(1)}, f32[1,4864]{1,0:T(1,128)S(1)}, u32[]{:S(2)}, u32[]{:S(2)}) %collective-permute-start.8) | collective-permute-done | bytes 19488 | tf_op jit(solution)/shard_map/ppermute | solution.py:52
  31.6 2.4 %collective-permute-start.10 = (f32[1,4864]{1,0:T(1,128)S(1)}, f32[1,4864]{1,0:T(1,128)S(1)}, u32[]{:S(2)}, u32[]{:S(2)}) collective-permute-start(f32[1,4864]{1,0:T(1,128)S(1)} %shard_map.105.own), channel_id=1, source_target_pairs={{0,96},{4,100},{8,104},{12,108},{16,112},{20,116},{24,120},{28,124... | collective-permute-start | bytes 58376 | tf_op jit(solution)/shard_map/ppermute | solution.py:52
  33.9 4.4 %collective-permute-done.10.minus = f32[1,4864]{1,0:T(1,128)S(1)} collective-permute-done((f32[1,4864]{1,0:T(1,128)S(1)}, f32[1,4864]{1,0:T(1,128)S(1)}, u32[]{:S(2)}, u32[]{:S(2)}) %collective-permute-start.10) | collective-permute-done | bytes 19488 | tf_op jit(solution)/shard_map/ppermute | solution.py:52
  38.3 3.0 %collective-permute-start.11 = (f32[1,4864]{1,0:T(1,128)S(1)}, f32[1,4864]{1,0:T(1,128)S(1)}, u32[]{:S(2)}, u32[]{:S(2)}) collective-permute-start(f32[1,4864]{1,0:T(1,128)S(1)} %shard_map.105.own), channel_id=1, source_target_pairs={{0,64},{4,68},{8,72},{12,76},{16,80},{20,84},{24,88},{28,92},{32,9... | collective-permute-start | bytes 58376 | tf_op jit(solution)/shard_map/ppermute | solution.py:52
  41.3 1.7 %collective-permute-done.11.far = f32[1,4864]{1,0:T(1,128)S(1)} collective-permute-done((f32[1,4864]{1,0:T(1,128)S(1)}, f32[1,4864]{1,0:T(1,128)S(1)}, u32[]{:S(2)}, u32[]{:S(2)}) %collective-permute-start.11) | collective-permute-done | bytes 19488 | tf_op jit(solution)/shard_map/ppermute | solution.py:52
  43.0 1.2 collective-permute-start.9
  44.1 2.7 %collective-permute-done.9.plus = f32[1,4864]{1,0:T(1,128)S(1)} collective-permute-done((f32[1,4864]{1,0:T(1,128)S(1)}, f32[1,4864]{1,0:T(1,128)S(1)}, u32[]{:S(2)}, u32[]{:S(2)}) %collective-permute-start.9) | collective-permute-done | bytes 19488 | tf_op jit(solution)/shard_map/ppermute | solution.py:52
  46.8 1.1 copy-done.1
  47.9 2.7 %shard_map.109 = (bf16[2560,2432]{1,0:T(8,128)(2,1)}, bf16[2560,2432]{1,0:T(8,128)(2,1)}, bf16[2,80,4864]{2,1,0:T(8,128)(2,1)S(1)}) custom-call(bf16[80,4992]{1,0:T(8,128)(2,1)} %get-tuple-element.36.block.refs_0_, bf16[80,4992]{1,0:T(8,128)(2,1)S(1)} %collective-permute-done.13.a.refs_1_, bf16[64,4864]{1,0:T(8,128)(2,1)S(1)} %copy-done.1, ...), custom_call_target="tpu_custom_call" | custom-call | flops 6000000 | bytes 1 | tf_op jit(solution)/shard_map/pallas_call | solution.py:235
  50.6 1.6 %collective-permute-start.17 = (bf16[2,80,4864]{2,1,0:T(8,128)(2,1)S(1)}, bf16[2,80,4864]{2,1,0:T(8,128)(2,1)S(1)}, u32[]{:S(2)}, u32[]{:S(2)}) collective-permute-start(bf16[2,80,4864]{2,1,0:T(8,128)(2,1)S(1)} %get-tuple-element.41), channel_id=1, source_target_pairs={{0,4},{4,0},{8,12},{12,8},{16,20},{20,16},{24,28},{28,24},{32,36},... | collective-permute-start | bytes 4669448 | tf_op jit(solution)/shard_map/ppermute | solution.py:52
  52.3 1.1 copy-done.2
  53.4 1.6 %shard_map.110 = (bf16[2560,2432]{1,0:T(8,128)(2,1)}, bf16[2560,2432]{1,0:T(8,128)(2,1)}, bf16[2,80,4864]{2,1,0:T(8,128)(2,1)S(1)}) custom-call(bf16[80,4992]{1,0:T(8,128)(2,1)S(1)} %collective-permute-done.refs_0_, bf16[80,4992]{1,0:T(8,128)(2,1)S(1)} %collective-permute-done.18.refs_1_, ...), custom_call_target="tpu_custom_call", output_to_operand_aliasing={{0}: (4, {}), {1}: (5, {})} | custom-call | flops 6000000 | bytes 1 | tf_op jit(solution)/shard_map/pallas_call | solution.py:235
  55.0 0.1 collective-permute-start.21
  55.1 0.1 shard_map.107
  55.1 1.7 %collective-permute-start.16 = (bf16[32,4992]{1,0:T(8,128)(2,1)S(1)}, bf16[32,4992]{1,0:T(8,128)(2,1)S(1)}, u32[]{:S(2)}, u32[]{:S(2)}) collective-permute-start(bf16[32,4992]{1,0:T(8,128)(2,1)S(1)} %get-tuple-element.40), channel_id=1, source_target_pairs={{0,24},{4,100},{8,0},{12,108},{16,8},{20,116},{24,16},{28,124},{32... | collective-permute-start | bytes 958472 | tf_op jit(solution)/shard_map/ppermute | solution.py:52
  56.8 6.7 %collective-permute-start.20 = (bf16[80,4992]{1,0:T(8,128)(2,1)S(1)}, bf16[80,4992]{1,0:T(8,128)(2,1)S(1)}, u32[]{:S(2)}, u32[]{:S(2)}) collective-permute-start(bf16[80,4992]{1,0:T(8,128)(2,1)S(1)} %collective-permute-done.13.a.refs_1_), channel_id=1, source_target_pairs={{0,32},{4,12},{8,40},{12,20},{16,48},{20,28},{24,56},{28,4},{32,64... | collective-permute-start | bytes 2396168 | tf_op jit(solution)/shard_map/ppermute | solution.py:52
  63.5 1.6 %collective-permute-start.3 = (bf16[80,4992]{1,0:T(8,128)(2,1)S(1)}, bf16[80,4992]{1,0:T(8,128)(2,1)S(1)}, u32[]{:S(2)}, u32[]{:S(2)}) collective-permute-start(bf16[80,4992]{1,0:T(8,128)(2,1)S(1)} %collective-permute-done.2.b.refs_0_), channel_id=1, source_target_pairs={{0,96},{4,28},{8,104},{12,4},{16,112},{20,12},{24,120},{28,20},{32... | collective-permute-start | bytes 2396168 | tf_op jit(solution)/shard_map/ppermute | solution.py:52
  65.1 0.0 collective-permute-start.15
  65.1 14.2 %collective-permute-done.15.top = bf16[48,4992]{1,0:T(8,128)(2,1)S(1)} collective-permute-done((bf16[48,4992]{1,0:T(8,128)(2,1)S(1)}, bf16[48,4992]{1,0:T(8,128)(2,1)S(1)}, u32[]{:S(2)}, u32[]{:S(2)}) %collective-permute-start.15) | collective-permute-done | bytes 479264 | tf_op jit(solution)/shard_map/ppermute | solution.py:52
  79.2 0.9 collective-permute-start.12
  80.1 0.1 shard_map.108.refs_1_
  80.2 1.8 %shard_map.111 = (bf16[2560,2432]{1,0:T(8,128)(2,1)}, bf16[2560,2432]{1,0:T(8,128)(2,1)}, bf16[2,80,4864]{2,1,0:T(8,128)(2,1)S(1)}) custom-call(bf16[80,4992]{1,0:T(8,128)(2,1)S(1)} %collective-permute-done.2.b.refs_0_, bf16[80,4992]{1,0:T(8,128)(2,1)S(1)} %shard_map.108.refs_1_, ...), custom_call_target="tpu_custom_call", output_to_operand_aliasing={{0}: (5, {}), {1}: (6, {})} | custom-call | flops 6000000 | bytes 1 | tf_op jit(solution)/shard_map/pallas_call | solution.py:235
  81.9 1.6 %collective-permute-start.19 = (bf16[2,80,4864]{2,1,0:T(8,128)(2,1)S(1)}, bf16[2,80,4864]{2,1,0:T(8,128)(2,1)S(1)}, u32[]{:S(2)}, u32[]{:S(2)}) collective-permute-start(bf16[2,80,4864]{2,1,0:T(8,128)(2,1)S(1)} %get-tuple-element.46), channel_id=1, source_target_pairs={{0,4},{4,0},{8,12},{12,8},{16,20},{20,16},{24,28},{28,24},{32,36},... | collective-permute-start | bytes 4669448 | tf_op jit(solution)/shard_map/ppermute | solution.py:52
  83.6 0.0 collective-permute-done.20.refs_0_
  83.6 1.8 %shard_map.112 = (bf16[2560,2432]{1,0:T(8,128)(2,1)}, bf16[2560,2432]{1,0:T(8,128)(2,1)}, bf16[2,80,4864]{2,1,0:T(8,128)(2,1)S(1)}) custom-call(bf16[80,4992]{1,0:T(8,128)(2,1)S(1)} %collective-permute-done.20.refs_0_, bf16[80,4992]{1,0:T(8,128)(2,1)S(1)} %collective-permute-done.3.refs_1_, ...), custom_call_target="tpu_custom_call", output_to_operand_aliasing={{0}: (5, {}), {1}: (6, {})} | custom-call | flops 6000000 | bytes 1 | tf_op jit(solution)/shard_map/pallas_call | solution.py:235
  85.3 0.1 collective-permute-start.25
  85.5 1.8 %collective-permute-start.14 = (bf16[80,4992]{1,0:T(8,128)(2,1)S(1)}, bf16[80,4992]{1,0:T(8,128)(2,1)S(1)}, u32[]{:S(2)}, u32[]{:S(2)}) collective-permute-start(bf16[80,4992]{1,0:T(8,128)(2,1)S(1)} %collective-permute-done.13.a.refs_1_), channel_id=1, source_target_pairs={{0,96},{4,28},{8,104},{12,4},{16,112},{20,12},{24,120},{28,20},{32... | collective-permute-start | bytes 2396168 | tf_op jit(solution)/shard_map/ppermute | solution.py:52
  87.2 0.1 collective-permute-start.24
  87.4 4.3 %collective-permute-done.12.refs_0_ = bf16[80,4992]{1,0:T(8,128)(2,1)S(1)} collective-permute-done((bf16[80,4992]{1,0:T(8,128)(2,1)S(1)}, bf16[80,4992]{1,0:T(8,128)(2,1)S(1)}, u32[]{:S(2)}, u32[]{:S(2)}) %collective-permute-start.12) | collective-permute-done | bytes 798752 | tf_op jit(solution)/shard_map/ppermute | solution.py:52
  91.7 5.1 %collective-permute-done.14.refs_1_ = bf16[80,4992]{1,0:T(8,128)(2,1)S(1)} collective-permute-done((bf16[80,4992]{1,0:T(8,128)(2,1)S(1)}, bf16[80,4992]{1,0:T(8,128)(2,1)S(1)}, u32[]{:S(2)}, u32[]{:S(2)}) %collective-permute-start.14) | collective-permute-done | bytes 798752 | tf_op jit(solution)/shard_map/ppermute | solution.py:52
  96.8 0.0 collective-permute-start.1
  96.8 1.7 %shard_map.113 = (bf16[2560,2432]{1,0:T(8,128)(2,1)}, bf16[2560,2432]{1,0:T(8,128)(2,1)}, bf16[2,80,4864]{2,1,0:T(8,128)(2,1)S(1)}) custom-call(bf16[80,4992]{1,0:T(8,128)(2,1)S(1)} %collective-permute-done.12.refs_0_, bf16[80,4992]{1,0:T(8,128)(2,1)S(1)} %collective-permute-done.14.refs_1_, ...), custom_call_target="tpu_custom_call", output_to_operand_aliasing={{0}: (5, {}), {1}: (6, {})} | custom-call | flops 6000000 | bytes 1 | tf_op jit(solution)/shard_map/pallas_call | solution.py:235
  98.5 3.7 %collective-permute-start.22 = (bf16[2,80,4864]{2,1,0:T(8,128)(2,1)S(1)}, bf16[2,80,4864]{2,1,0:T(8,128)(2,1)S(1)}, u32[]{:S(2)}, u32[]{:S(2)}) collective-permute-start(bf16[2,80,4864]{2,1,0:T(8,128)(2,1)S(1)} %get-tuple-element.52), channel_id=1, source_target_pairs={{0,4},{4,0},{8,12},{12,8},{16,20},{20,16},{24,28},{28,24},{32,36},... | collective-permute-start | bytes 4669448 | tf_op jit(solution)/shard_map/ppermute | solution.py:52
  102.3 3.1 %collective-permute-done.24.refs_1_ = bf16[80,4992]{1,0:T(8,128)(2,1)S(1)} collective-permute-done((bf16[80,4992]{1,0:T(8,128)(2,1)S(1)}, bf16[80,4992]{1,0:T(8,128)(2,1)S(1)}, u32[]{:S(2)}, u32[]{:S(2)}) %collective-permute-start.24) | collective-permute-done | bytes 798752 | tf_op jit(solution)/shard_map/ppermute | solution.py:52
  105.3 1.7 %shard_map.114 = (bf16[2560,2432]{1,0:T(8,128)(2,1)}, bf16[2560,2432]{1,0:T(8,128)(2,1)}, bf16[2,80,4864]{2,1,0:T(8,128)(2,1)S(1)}) custom-call(bf16[80,4992]{1,0:T(8,128)(2,1)S(1)} %collective-permute-done.23.refs_0_, bf16[80,4992]{1,0:T(8,128)(2,1)S(1)} %collective-permute-done.24.refs_1_, ...), custom_call_target="tpu_custom_call", output_to_operand_aliasing={{0}: (5, {}), {1}: (6, {})} | custom-call | flops 6000000 | bytes 1 | tf_op jit(solution)/shard_map/pallas_call | solution.py:235
  107.1 3.0 %collective-permute-start.29 = (bf16[2,80,4864]{2,1,0:T(8,128)(2,1)S(1)}, bf16[2,80,4864]{2,1,0:T(8,128)(2,1)S(1)}, u32[]{:S(2)}, u32[]{:S(2)}) collective-permute-start(bf16[2,80,4864]{2,1,0:T(8,128)(2,1)S(1)} %get-tuple-element.59), channel_id=1, source_target_pairs={{0,4},{4,0},{8,12},{12,8},{16,20},{20,16},{24,28},{28,24},{32,36},... | collective-permute-start | bytes 4669448 | tf_op jit(solution)/shard_map/ppermute | solution.py:52
  110.1 1.7 %collective-permute-start.4 = (bf16[80,4992]{1,0:T(8,128)(2,1)S(1)}, bf16[80,4992]{1,0:T(8,128)(2,1)S(1)}, u32[]{:S(2)}, u32[]{:S(2)}) collective-permute-start(bf16[80,4992]{1,0:T(8,128)(2,1)S(1)} %collective-permute-done.3.refs_1_), channel_id=1, source_target_pairs={{0,96},{4,28},{8,104},{12,4},{16,112},{20,12},{24,120},{28,20},{32... | collective-permute-start | bytes 2396168 | tf_op jit(solution)/shard_map/ppermute | solution.py:52
  111.8 0.9 collective-permute-done.1.refs_0_
  112.8 1.7 %collective-permute-start.28 = (bf16[80,4992]{1,0:T(8,128)(2,1)S(1)}, bf16[80,4992]{1,0:T(8,128)(2,1)S(1)}, u32[]{:S(2)}, u32[]{:S(2)}) collective-permute-start(bf16[80,4992]{1,0:T(8,128)(2,1)S(1)} %collective-permute-done.24.refs_1_), channel_id=1, source_target_pairs={{0,96},{4,28},{8,104},{12,4},{16,112},{20,12},{24,120},{28,20},{32... | collective-permute-start | bytes 2396168 | tf_op jit(solution)/shard_map/ppermute | solution.py:52
  114.5 6.8 %collective-permute-done.4.refs_1_ = bf16[80,4992]{1,0:T(8,128)(2,1)S(1)} collective-permute-done((bf16[80,4992]{1,0:T(8,128)(2,1)S(1)}, bf16[80,4992]{1,0:T(8,128)(2,1)S(1)}, u32[]{:S(2)}, u32[]{:S(2)}) %collective-permute-start.4) | collective-permute-done | bytes 798752 | tf_op jit(solution)/shard_map/ppermute | solution.py:52
  121.3 1.7 %shard_map.115 = (bf16[2560,2432]{1,0:T(8,128)(2,1)}, bf16[2560,2432]{1,0:T(8,128)(2,1)}, bf16[2,80,4864]{2,1,0:T(8,128)(2,1)S(1)}) custom-call(bf16[80,4992]{1,0:T(8,128)(2,1)S(1)} %collective-permute-done.1.refs_0_, bf16[80,4992]{1,0:T(8,128)(2,1)S(1)} %collective-permute-done.4.refs_1_, ...), custom_call_target="tpu_custom_call", output_to_operand_aliasing={{0}: (5, {}), {1}: (6, {})} | custom-call | flops 6000000 | bytes 1 | tf_op jit(solution)/shard_map/pallas_call | solution.py:235
  123.1 1.2 collective-permute-done.27.refs_0_
  124.3 5.6 %collective-permute-done.28.refs_1_ = bf16[80,4992]{1,0:T(8,128)(2,1)S(1)} collective-permute-done((bf16[80,4992]{1,0:T(8,128)(2,1)S(1)}, bf16[80,4992]{1,0:T(8,128)(2,1)S(1)}, u32[]{:S(2)}, u32[]{:S(2)}) %collective-permute-start.28) | collective-permute-done | bytes 798752 | tf_op jit(solution)/shard_map/ppermute | solution.py:52
  129.9 1.8 %shard_map.116 = (bf16[2560,2432]{1,0:T(8,128)(2,1)}, bf16[2560,2432]{1,0:T(8,128)(2,1)}, bf16[2,80,4864]{2,1,0:T(8,128)(2,1)S(1)}) custom-call(bf16[80,4992]{1,0:T(8,128)(2,1)S(1)} %collective-permute-done.27.refs_0_, bf16[80,4992]{1,0:T(8,128)(2,1)S(1)} %collective-permute-done.28.refs_1_, ...), custom_call_target="tpu_custom_call", output_to_operand_aliasing={{0}: (5, {}), {1}: (6, {})} | custom-call | flops 6000000 | bytes 1 | tf_op jit(solution)/shard_map/pallas_call | solution.py:235
  131.7 1.3 collective-permute-start.30
  132.9 0.1 collective-permute-start.26
  133.0 0.6 slice_reduce_fusion
  133.7 2.3 %collective-permute-done.30.refs_1_ = bf16[2,80,4864]{2,1,0:T(8,128)(2,1)S(1)} collective-permute-done((bf16[2,80,4864]{2,1,0:T(8,128)(2,1)S(1)}, bf16[2,80,4864]{2,1,0:T(8,128)(2,1)S(1)}, u32[]{:S(2)}, u32[]{:S(2)}) %collective-permute-start.30) | collective-permute-done | bytes 1556512 | tf_op jit(solution)/shard_map/ppermute | solution.py:52
  135.9 2.2 %collective-permute-done.26.refs_0_ = bf16[2,80,4864]{2,1,0:T(8,128)(2,1)S(1)} collective-permute-done((bf16[2,80,4864]{2,1,0:T(8,128)(2,1)S(1)}, bf16[2,80,4864]{2,1,0:T(8,128)(2,1)S(1)}, u32[]{:S(2)}, u32[]{:S(2)}) %collective-permute-start.26) | collective-permute-done | bytes 1556512 | tf_op jit(solution)/shard_map/ppermute | solution.py:52
  138.2 1.7 %shard_map.117 = (bf16[2560,2432]{1,0:T(8,128)(2,1)}, bf16[2560,2432]{1,0:T(8,128)(2,1)}) custom-call(bf16[2,80,4864]{2,1,0:T(8,128)(2,1)S(1)} %collective-permute-done.26.refs_0_, bf16[2,80,4864]{2,1,0:T(8,128)(2,1)S(1)} %collective-permute-done.30.refs_1_, ...), custom_call_target="tpu_custom_call", output_to_operand_aliasing={{0}: (2, {}), {1}: (3, {})} | custom-call | flops 4000000 | bytes 1 | tf_op jit(solution)/shard_map/pallas_call | solution.py:249
  (21 shorter events, 0.1 us)
Async XLA Ops:
  3.1 43.7 %collective-permute-start.13 = (bf16[80,4992]{1,0:T(8,128)(2,1)}, bf16[80,4992]{1,0:T(8,128)(2,1)S(1)}, u32[]{:S(2)}, u32[]{:S(2)}) collective-permute-start(bf16[80,4992]{1,0:T(8,128)(2,1)} %get-tuple-element.36.block.refs_0_), channel_id=1, source_target_pairs={{0,8},{4,36},{8,16},{12,44},{16,24},{20,52},{24,0},{28,60},{32,40}... | collective-permute-start | bytes 2396168 | tf_op jit(solution)/shard_map/ppermute | solution.py:52
  5.3 47.0 %collective-permute-start = (bf16[80,4992]{1,0:T(8,128)(2,1)}, bf16[80,4992]{1,0:T(8,128)(2,1)S(1)}, u32[]{:S(2)}, u32[]{:S(2)}) collective-permute-start(bf16[80,4992]{1,0:T(8,128)(2,1)} %get-tuple-element.36.block.refs_0_), channel_id=1, source_target_pairs={{0,32},{4,12},{8,40},{12,20},{16,48},{20,28},{24,56},{28,4},{32,64... | collective-permute-start | bytes 2396168 | tf_op jit(solution)/shard_map/ppermute | solution.py:52
  6.5 45.8 %collective-permute-start.18 = (bf16[80,4992]{1,0:T(8,128)(2,1)}, bf16[80,4992]{1,0:T(8,128)(2,1)S(1)}, u32[]{:S(2)}, u32[]{:S(2)}) collective-permute-start(bf16[80,4992]{1,0:T(8,128)(2,1)} %get-tuple-element.36.block.refs_0_), channel_id=1, source_target_pairs={{0,96},{4,28},{8,104},{12,4},{16,112},{20,12},{24,120},{28,20},{32... | collective-permute-start | bytes 2396168 | tf_op jit(solution)/shard_map/ppermute | solution.py:52
  8.0 1.1 copy-start
  10.6 2.4 %collective-permute-start.5 = (f32[1,4864]{1,0:T(1,128)S(1)}, f32[1,4864]{1,0:T(1,128)S(1)}, u32[]{:S(2)}, u32[]{:S(2)}) collective-permute-start(f32[1,4864]{1,0:T(1,128)S(1)} %shard_map.103.a), channel_id=1, source_target_pairs={{0,4},{4,0},{8,12},{12,8},{16,20},{20,16},{24,28},{28,24},{32,36},... | collective-permute-start | bytes 58376 | tf_op jit(solution)/shard_map/ppermute | solution.py:52
  13.0 13.4 %collective-permute-start.6 = (f32[1,4864]{1,0:T(1,128)S(1)}, f32[1,4864]{1,0:T(1,128)S(1)}, u32[]{:S(2)}, u32[]{:S(2)}) collective-permute-start(f32[1,4864]{1,0:T(1,128)S(1)} %shard_map.104.own), channel_id=1, source_target_pairs={{0,8},{4,12},{8,16},{12,20},{16,24},{20,28},{24,0},{28,4},{32,40},... | collective-permute-start | bytes 58376 | tf_op jit(solution)/shard_map/ppermute | solution.py:52
  14.2 13.2 %collective-permute-start.7 = (f32[1,4864]{1,0:T(1,128)S(1)}, f32[1,4864]{1,0:T(1,128)S(1)}, u32[]{:S(2)}, u32[]{:S(2)}) collective-permute-start(f32[1,4864]{1,0:T(1,128)S(1)} %shard_map.104.own), channel_id=1, source_target_pairs={{0,24},{4,28},{8,0},{12,4},{16,8},{20,12},{24,16},{28,20},{32,56},... | collective-permute-start | bytes 58376 | tf_op jit(solution)/shard_map/ppermute | solution.py:52
  26.4 28.7 %collective-permute-start.2 = (bf16[80,4992]{1,0:T(8,128)(2,1)}, bf16[80,4992]{1,0:T(8,128)(2,1)S(1)}, u32[]{:S(2)}, u32[]{:S(2)}) collective-permute-start(bf16[80,4992]{1,0:T(8,128)(2,1)} %get-tuple-element.36.block.refs_0_), channel_id=1, source_target_pairs={{0,24},{4,100},{8,0},{12,108},{16,8},{20,116},{24,16},{28,124},{32... | collective-permute-start | bytes 2396168 | tf_op jit(solution)/shard_map/ppermute | solution.py:52
  27.4 4.1 %collective-permute-start.8 = (f32[1,4864]{1,0:T(1,128)S(1)}, f32[1,4864]{1,0:T(1,128)S(1)}, u32[]{:S(2)}, u32[]{:S(2)}) collective-permute-start(f32[1,4864]{1,0:T(1,128)S(1)} %shard_map.104.own), channel_id=1, source_target_pairs={{0,16},{4,20},{8,24},{12,28},{16,0},{20,4},{24,8},{28,12},{32,48},... | collective-permute-start | bytes 58376 | tf_op jit(solution)/shard_map/ppermute | solution.py:52
  31.6 6.8 %collective-permute-start.10 = (f32[1,4864]{1,0:T(1,128)S(1)}, f32[1,4864]{1,0:T(1,128)S(1)}, u32[]{:S(2)}, u32[]{:S(2)}) collective-permute-start(f32[1,4864]{1,0:T(1,128)S(1)} %shard_map.105.own), channel_id=1, source_target_pairs={{0,96},{4,100},{8,104},{12,108},{16,112},{20,116},{24,120},{28,124... | collective-permute-start | bytes 58376 | tf_op jit(solution)/shard_map/ppermute | solution.py:52
  38.3 4.6 %collective-permute-start.11 = (f32[1,4864]{1,0:T(1,128)S(1)}, f32[1,4864]{1,0:T(1,128)S(1)}, u32[]{:S(2)}, u32[]{:S(2)}) collective-permute-start(f32[1,4864]{1,0:T(1,128)S(1)} %shard_map.105.own), channel_id=1, source_target_pairs={{0,64},{4,68},{8,72},{12,76},{16,80},{20,84},{24,88},{28,92},{32,9... | collective-permute-start | bytes 58376 | tf_op jit(solution)/shard_map/ppermute | solution.py:52
  43.0 3.8 %collective-permute-start.9 = (f32[1,4864]{1,0:T(1,128)S(1)}, f32[1,4864]{1,0:T(1,128)S(1)}, u32[]{:S(2)}, u32[]{:S(2)}) collective-permute-start(f32[1,4864]{1,0:T(1,128)S(1)} %shard_map.105.own), channel_id=1, source_target_pairs={{0,32},{4,36},{8,40},{12,44},{16,48},{20,52},{24,56},{28,60},{32,6... | collective-permute-start | bytes 58376 | tf_op jit(solution)/shard_map/ppermute | solution.py:52
  46.8 1.1 copy-start.1
  50.6 29.5 %collective-permute-start.17 = (bf16[2,80,4864]{2,1,0:T(8,128)(2,1)S(1)}, bf16[2,80,4864]{2,1,0:T(8,128)(2,1)S(1)}, u32[]{:S(2)}, u32[]{:S(2)}) collective-permute-start(bf16[2,80,4864]{2,1,0:T(8,128)(2,1)S(1)} %get-tuple-element.41), channel_id=1, source_target_pairs={{0,4},{4,0},{8,12},{12,8},{16,20},{20,16},{24,28},{28,24},{32,36},... | collective-permute-start | bytes 4669448 | tf_op jit(solution)/shard_map/ppermute | solution.py:52
  52.3 1.1 copy-start.2
  55.0 28.6 %collective-permute-start.21 = (bf16[2,80,4864]{2,1,0:T(8,128)(2,1)S(1)}, bf16[2,80,4864]{2,1,0:T(8,128)(2,1)S(1)}, u32[]{:S(2)}, u32[]{:S(2)}) collective-permute-start(bf16[2,80,4864]{2,1,0:T(8,128)(2,1)S(1)} %get-tuple-element.47), channel_id=1, source_target_pairs={{0,4},{4,0},{8,12},{12,8},{16,20},{20,16},{24,28},{28,24},{32,36},... | collective-permute-start | bytes 4669448 | tf_op jit(solution)/shard_map/ppermute | solution.py:52
  55.1 9.9 %collective-permute-start.16 = (bf16[32,4992]{1,0:T(8,128)(2,1)S(1)}, bf16[32,4992]{1,0:T(8,128)(2,1)S(1)}, u32[]{:S(2)}, u32[]{:S(2)}) collective-permute-start(bf16[32,4992]{1,0:T(8,128)(2,1)S(1)} %get-tuple-element.40), channel_id=1, source_target_pairs={{0,24},{4,100},{8,0},{12,108},{16,8},{20,116},{24,16},{28,124},{32... | collective-permute-start | bytes 958472 | tf_op jit(solution)/shard_map/ppermute | solution.py:52
  56.8 26.8 %collective-permute-start.20 = (bf16[80,4992]{1,0:T(8,128)(2,1)S(1)}, bf16[80,4992]{1,0:T(8,128)(2,1)S(1)}, u32[]{:S(2)}, u32[]{:S(2)}) collective-permute-start(bf16[80,4992]{1,0:T(8,128)(2,1)S(1)} %collective-permute-done.13.a.refs_1_), channel_id=1, source_target_pairs={{0,32},{4,12},{8,40},{12,20},{16,48},{20,28},{24,56},{28,4},{32,64... | collective-permute-start | bytes 2396168 | tf_op jit(solution)/shard_map/ppermute | solution.py:52
  63.5 20.1 %collective-permute-start.3 = (bf16[80,4992]{1,0:T(8,128)(2,1)S(1)}, bf16[80,4992]{1,0:T(8,128)(2,1)S(1)}, u32[]{:S(2)}, u32[]{:S(2)}) collective-permute-start(bf16[80,4992]{1,0:T(8,128)(2,1)S(1)} %collective-permute-done.2.b.refs_0_), channel_id=1, source_target_pairs={{0,96},{4,28},{8,104},{12,4},{16,112},{20,12},{24,120},{28,20},{32... | collective-permute-start | bytes 2396168 | tf_op jit(solution)/shard_map/ppermute | solution.py:52
  65.1 14.2 %collective-permute-start.15 = (bf16[48,4992]{1,0:T(8,128)(2,1)S(1)}, bf16[48,4992]{1,0:T(8,128)(2,1)S(1)}, u32[]{:S(2)}, u32[]{:S(2)}) collective-permute-start(bf16[48,4992]{1,0:T(8,128)(2,1)S(1)} %get-tuple-element.39), channel_id=1, source_target_pairs={{0,8},{4,36},{8,16},{12,44},{16,24},{20,52},{24,0},{28,60},{32,40}... | collective-permute-start | bytes 1437704 | tf_op jit(solution)/shard_map/ppermute | solution.py:52
  79.2 12.5 %collective-permute-start.12 = (bf16[80,4992]{1,0:T(8,128)(2,1)S(1)}, bf16[80,4992]{1,0:T(8,128)(2,1)S(1)}, u32[]{:S(2)}, u32[]{:S(2)}) collective-permute-start(bf16[80,4992]{1,0:T(8,128)(2,1)S(1)} %collective-permute-done.2.b.refs_0_), channel_id=1, source_target_pairs={{0,32},{4,12},{8,40},{12,20},{16,48},{20,28},{24,56},{28,4},{32,64... | collective-permute-start | bytes 2396168 | tf_op jit(solution)/shard_map/ppermute | solution.py:52
  81.9 14.9 %collective-permute-start.19 = (bf16[2,80,4864]{2,1,0:T(8,128)(2,1)S(1)}, bf16[2,80,4864]{2,1,0:T(8,128)(2,1)S(1)}, u32[]{:S(2)}, u32[]{:S(2)}) collective-permute-start(bf16[2,80,4864]{2,1,0:T(8,128)(2,1)S(1)} %get-tuple-element.46), channel_id=1, source_target_pairs={{0,4},{4,0},{8,12},{12,8},{16,20},{20,16},{24,28},{28,24},{32,36},... | collective-permute-start | bytes 4669448 | tf_op jit(solution)/shard_map/ppermute | solution.py:52
  85.3 20.0 %collective-permute-start.25 = (bf16[2,80,4864]{2,1,0:T(8,128)(2,1)S(1)}, bf16[2,80,4864]{2,1,0:T(8,128)(2,1)S(1)}, u32[]{:S(2)}, u32[]{:S(2)}) collective-permute-start(bf16[2,80,4864]{2,1,0:T(8,128)(2,1)S(1)} %get-tuple-element.53), channel_id=1, source_target_pairs={{0,4},{4,0},{8,12},{12,8},{16,20},{20,16},{24,28},{28,24},{32,36},... | collective-permute-start | bytes 4669448 | tf_op jit(solution)/shard_map/ppermute | solution.py:52
  85.5 11.3 %collective-permute-start.14 = (bf16[80,4992]{1,0:T(8,128)(2,1)S(1)}, bf16[80,4992]{1,0:T(8,128)(2,1)S(1)}, u32[]{:S(2)}, u32[]{:S(2)}) collective-permute-start(bf16[80,4992]{1,0:T(8,128)(2,1)S(1)} %collective-permute-done.13.a.refs_1_), channel_id=1, source_target_pairs={{0,96},{4,28},{8,104},{12,4},{16,112},{20,12},{24,120},{28,20},{32... | collective-permute-start | bytes 2396168 | tf_op jit(solution)/shard_map/ppermute | solution.py:52
  87.2 18.1 %collective-permute-start.24 = (bf16[80,4992]{1,0:T(8,128)(2,1)S(1)}, bf16[80,4992]{1,0:T(8,128)(2,1)S(1)}, u32[]{:S(2)}, u32[]{:S(2)}) collective-permute-start(bf16[80,4992]{1,0:T(8,128)(2,1)S(1)} %shard_map.108.refs_1_), channel_id=1, source_target_pairs={{0,96},{4,28},{8,104},{12,4},{16,112},{20,12},{24,120},{28,20},{32... | collective-permute-start | bytes 2396168 | tf_op jit(solution)/shard_map/ppermute | solution.py:52
  91.7 13.6 %collective-permute-start.23 = (bf16[80,4992]{1,0:T(8,128)(2,1)S(1)}, bf16[80,4992]{1,0:T(8,128)(2,1)S(1)}, u32[]{:S(2)}, u32[]{:S(2)}) collective-permute-start(bf16[80,4992]{1,0:T(8,128)(2,1)S(1)} %shard_map.108.refs_1_), channel_id=1, source_target_pairs={{0,32},{4,12},{8,40},{12,20},{16,48},{20,28},{24,56},{28,4},{32,64... | collective-permute-start | bytes 2396168 | tf_op jit(solution)/shard_map/ppermute | solution.py:52
  96.8 16.0 %collective-permute-start.1 = (bf16[80,4992]{1,0:T(8,128)(2,1)S(1)}, bf16[80,4992]{1,0:T(8,128)(2,1)S(1)}, u32[]{:S(2)}, u32[]{:S(2)}) collective-permute-start(bf16[80,4992]{1,0:T(8,128)(2,1)S(1)} %collective-permute-done.refs_0_), channel_id=1, source_target_pairs={{0,32},{4,12},{8,40},{12,20},{16,48},{20,28},{24,56},{28,4},{32,64... | collective-permute-start | bytes 2396168 | tf_op jit(solution)/shard_map/ppermute | solution.py:52
  98.5 22.8 %collective-permute-start.22 = (bf16[2,80,4864]{2,1,0:T(8,128)(2,1)S(1)}, bf16[2,80,4864]{2,1,0:T(8,128)(2,1)S(1)}, u32[]{:S(2)}, u32[]{:S(2)}) collective-permute-start(bf16[2,80,4864]{2,1,0:T(8,128)(2,1)S(1)} %get-tuple-element.52), channel_id=1, source_target_pairs={{0,4},{4,0},{8,12},{12,8},{16,20},{20,16},{24,28},{28,24},{32,36},... | collective-permute-start | bytes 4669448 | tf_op jit(solution)/shard_map/ppermute | solution.py:52
  107.1 22.8 %collective-permute-start.29 = (bf16[2,80,4864]{2,1,0:T(8,128)(2,1)S(1)}, bf16[2,80,4864]{2,1,0:T(8,128)(2,1)S(1)}, u32[]{:S(2)}, u32[]{:S(2)}) collective-permute-start(bf16[2,80,4864]{2,1,0:T(8,128)(2,1)S(1)} %get-tuple-element.59), channel_id=1, source_target_pairs={{0,4},{4,0},{8,12},{12,8},{16,20},{20,16},{24,28},{28,24},{32,36},... | collective-permute-start | bytes 4669448 | tf_op jit(solution)/shard_map/ppermute | solution.py:52
  110.1 11.3 %collective-permute-start.4 = (bf16[80,4992]{1,0:T(8,128)(2,1)S(1)}, bf16[80,4992]{1,0:T(8,128)(2,1)S(1)}, u32[]{:S(2)}, u32[]{:S(2)}) collective-permute-start(bf16[80,4992]{1,0:T(8,128)(2,1)S(1)} %collective-permute-done.3.refs_1_), channel_id=1, source_target_pairs={{0,96},{4,28},{8,104},{12,4},{16,112},{20,12},{24,120},{28,20},{32... | collective-permute-start | bytes 2396168 | tf_op jit(solution)/shard_map/ppermute | solution.py:52
  111.8 12.5 %collective-permute-start.27 = (bf16[80,4992]{1,0:T(8,128)(2,1)S(1)}, bf16[80,4992]{1,0:T(8,128)(2,1)S(1)}, u32[]{:S(2)}, u32[]{:S(2)}) collective-permute-start(bf16[80,4992]{1,0:T(8,128)(2,1)S(1)} %collective-permute-done.20.refs_0_), channel_id=1, source_target_pairs={{0,32},{4,12},{8,40},{12,20},{16,48},{20,28},{24,56},{28,4},{32,64... | collective-permute-start | bytes 2396168 | tf_op jit(solution)/shard_map/ppermute | solution.py:52
  112.8 17.1 %collective-permute-start.28 = (bf16[80,4992]{1,0:T(8,128)(2,1)S(1)}, bf16[80,4992]{1,0:T(8,128)(2,1)S(1)}, u32[]{:S(2)}, u32[]{:S(2)}) collective-permute-start(bf16[80,4992]{1,0:T(8,128)(2,1)S(1)} %collective-permute-done.24.refs_1_), channel_id=1, source_target_pairs={{0,96},{4,28},{8,104},{12,4},{16,112},{20,12},{24,120},{28,20},{32... | collective-permute-start | bytes 2396168 | tf_op jit(solution)/shard_map/ppermute | solution.py:52
  131.7 4.3 %collective-permute-start.30 = (bf16[2,80,4864]{2,1,0:T(8,128)(2,1)S(1)}, bf16[2,80,4864]{2,1,0:T(8,128)(2,1)S(1)}, u32[]{:S(2)}, u32[]{:S(2)}) collective-permute-start(bf16[2,80,4864]{2,1,0:T(8,128)(2,1)S(1)} %get-tuple-element.62), channel_id=1, source_target_pairs={{0,4},{4,0},{8,12},{12,8},{16,20},{20,16},{24,28},{28,24},{32,36},... | collective-permute-start | bytes 4669448 | tf_op jit(solution)/shard_map/ppermute | solution.py:52
  132.9 5.2 %collective-permute-start.26 = (bf16[2,80,4864]{2,1,0:T(8,128)(2,1)S(1)}, bf16[2,80,4864]{2,1,0:T(8,128)(2,1)S(1)}, u32[]{:S(2)}, u32[]{:S(2)}) collective-permute-start(bf16[2,80,4864]{2,1,0:T(8,128)(2,1)S(1)} %get-tuple-element.58), channel_id=1, source_target_pairs={{0,4},{4,0},{8,12},{12,8},{16,20},{20,16},{24,28},{28,24},{32,36},... | collective-permute-start | bytes 4669448 | tf_op jit(solution)/shard_map/ppermute | solution.py:52

commit v2 on v1

--- a/solution.py
+++ b/solution.py
@@ -33,11 +33,9 @@
     ]
 
 
-FIRST = {1: hops((0, 1), (1, 0)), -1: hops((0, -1), (-1, 0))}
-SECOND = {1: hops((1, 0), (0, 1)), -1: hops((-1, 0), (0, -1))}
+FIRST = {d: hops((0, d), (d, 0)) for d in (1, -1, 2)}
+SECOND = {d: hops((d, 0), (0, d)) for d in (1, -1, 2)}
 SIDE = hops((0, 0), (0, 0), 1)
-ALONG_X = {d: hops((0, d), (0, d)) for d in (1, -1, 2)}
-ALONG_Y = {d: hops((d, 0), (d, 0)) for d in (1, -1, 2)}
 
 
 def source(first, second, flip):
@@ -106,21 +104,19 @@
         sums[:, cols] = jnp.sum(v * v, axis=0, keepdims=True)
 
 
-def add_kernel(a, b, total):
-    total[...] = a[...] + b[...]
-
-
-def ring_kernel(bit, own, plus, minus, far, *outs):
-    even = ((lax.axis_index("shard") >> bit) & 1) == 0
+def ring_kernel(bits, own, plus, minus, far, total):
+    me = lax.axis_index("shard")
+    bit = jnp.where((me & 1) == 0, bits[0], bits[1])
+    even = ((me >> bit) & 1) == 0
     p, m = plus[...], minus[...]
     partner, other = jnp.where(even, m, p), jnp.where(even, p, m)
-    total = (own[...] + partner) + (other + far[...])
-    if len(outs) == 1:
-        outs[0][...] = total
-        return
-    factor = jnp.sqrt(total)
-    outs[0][...] = factor
-    outs[1][...] = 1.0 / factor
+    total[...] = (own[...] + partner) + (other + far[...])
+
+
+def factor_kernel(mine, theirs, factor, inv):
+    root = jnp.sqrt(mine[...] + theirs[...])
+    factor[...] = root
+    inv[...] = 1.0 / root
 
 
 def halves_kernel(a, b, top, bottom):
@@ -133,28 +129,34 @@
     block[TOP:] = bottom[...]
 
 
-def merge_kernel(mine, theirs, *refs):
-    n, place = len(mine), len(theirs)
-    blocks, refs = refs[:n], refs[n:]
-    high, inv = refs[0], refs[1]
-    moved, refs = refs[2 : 2 + (place > 0)], refs[2 + (place > 0) :]
-    out_gate, out_up, ready, sems = refs[2:]
-    outs = (out_gate, out_up)
-    copies = []
-
-    def send(src, at, flip, h):
-        row = pl.multiple_of(source(*at, flip) * ROWS, ROWS)
+def placer(outs, sems, copies):
+    def send(src, at, start, flip, h):
+        count = src.shape[0]
+        row = pl.multiple_of(source(*at, flip) * ROWS + start, 16)
         copy = pltpu.make_async_copy(
             src.at[:, pl.ds(h * HALF, HALF)],
-            outs[h].at[pl.ds(row, ROWS), :],
+            outs[h].at[pl.ds(row, count), :],
             sems.at[len(copies)],
         )
         copy.start()
         copies.append(copy)
 
-    for k in range(place):
-        for h in range(2):
-            send(moved[0].at[k], theirs[k], 1, h)
+    return send
+
+
+def merge_kernel(mine, start, theirs, *refs):
+    n, place = len(mine), len(theirs)
+    blocks, refs = refs[:n], refs[n:]
+    high, inv = refs[0], refs[1]
+    moved, refs = refs[2 : 2 + place], refs[2 + place :]
+    out_gate, out_up, ready, sems = refs[2:]
+    count = ready.shape[1]
+    copies = []
+    send = placer((out_gate, out_up), sems, copies)
+    for (pair, first), ref in zip(theirs, moved):
+        for k, at in enumerate(pair):
+            for h in range(2):
+                send(ref.at[k], at, first, 1, h)
     extra = jnp.concatenate([b[:, WIDE:] for b in blocks], axis=0)
     gain = gain_of(extra)
     for j in range(WIDE // TILE):
@@ -162,33 +164,26 @@
         low_rank = jnp.dot(extra[:, :64], high[:, cols], preferred_element_type=jnp.float32)
         scale = inv[:, cols]
         for k in range(n):
-            rows = slice(k * ROWS, (k + 1) * ROWS)
+            rows = slice(k * count, (k + 1) * count)
             v = blocks[k][:, cols].astype(jnp.float32) + low_rank[rows]
             ready[k, :, cols] = (v * gain[rows] * scale).astype(jnp.bfloat16)
         if j == HALF // TILE:
             for k in range(n):
-                send(ready.at[k], mine[k], 0, 0)
+                send(ready.at[k], mine[k], start, 0, 0)
     for k in range(n):
-        send(ready.at[k], mine[k], 0, 1)
+        send(ready.at[k], mine[k], start, 0, 1)
     for copy in copies:
         copy.wait()
 
 
 def place_kernel(theirs, *refs):
     moved, refs = refs[: len(theirs)], refs[len(theirs) + 2 :]
-    outs, sems = refs[:2], refs[2]
     copies = []
-    for i, pair in enumerate(theirs):
+    send = placer(refs[:2], refs[2], copies)
+    for (pair, first), ref in zip(theirs, moved):
         for k, at in enumerate(pair):
-            row = pl.multiple_of(source(*at, 1) * ROWS, ROWS)
-            for h, out in enumerate(outs):
-                copy = pltpu.make_async_copy(
-                    moved[i].at[k, :, pl.ds(h * HALF, HALF)],
-                    out.at[pl.ds(row, ROWS), :],
-                    sems.at[len(copies)],
-                )
-                copy.start()
-                copies.append(copy)
+            for h in range(2):
+                send(ref.at[k], at, first, 1, h)
     for copy in copies:
         copy.wait()
 
@@ -217,7 +212,7 @@
     )(*operands)
 
 
-def merged(blocks, mine, theirs, high, inv, moved, outs):
+def merged(blocks, mine, start, theirs, high, inv, moved, outs):
     operands = [*blocks, high, inv, *moved]
     count = len(operands)
     aliases = {}
@@ -226,18 +221,19 @@
         outs = ()
 
         def body(*refs):
-            merge_kernel(mine, theirs, *refs[:count], None, None, *refs[count:])
+            merge_kernel(mine, start, theirs, *refs[:count], None, None, *refs[count:])
     else:
         aliases = {count: 0, count + 1: 1}
         specs = specs + [ANY, ANY]
-        body = functools.partial(merge_kernel, mine, theirs)
-    n = len(mine)
+        body = functools.partial(merge_kernel, mine, start, theirs)
+    n, rows = len(mine), blocks[0].shape[0]
+    copies = 2 * (n + sum(len(pair) for pair, _ in theirs))
     return pl.pallas_call(
         body,
-        out_shape=(OUT, OUT, jax.ShapeDtypeStruct((n, ROWS, WIDE), jnp.bfloat16)),
+        out_shape=(OUT, OUT, jax.ShapeDtypeStruct((n, rows, WIDE), jnp.bfloat16)),
         in_specs=specs,
         out_specs=(ANY, ANY, pl.BlockSpec(memory_space=pltpu.VMEM)),
-        scratch_shapes=[pltpu.SemaphoreType.DMA((2 * (n + len(theirs)),))],
+        scratch_shapes=[pltpu.SemaphoreType.DMA((copies,))],
         input_output_aliases=aliases,
         compiler_params=params(14),
         cost_estimate=cost(1.5),
@@ -246,12 +242,13 @@
 
 def placed(theirs, moved, outs):
     n = len(moved)
+    copies = 2 * sum(len(pair) for pair, _ in theirs)
     return pl.pallas_call(
         functools.partial(place_kernel, theirs),
         out_shape=(OUT, OUT),
         in_specs=in_vmem(n) + [ANY, ANY],
         out_specs=(ANY, ANY),
-        scratch_shapes=[pltpu.SemaphoreType.DMA((2 * sum(map(len, theirs)),))],
+        scratch_shapes=[pltpu.SemaphoreType.DMA((copies,))],
         input_output_aliases={n: 0, n + 1: 1},
         compiler_params=params(10),
         cost_estimate=cost(1.0),
@@ -266,14 +263,19 @@
     block, high = small(
         pack_kernel,
         (a_block, shape((2 * RANK, WIDE), jnp.bfloat16)),
-        62.4,
-        weight_gate,
-        weight_up,
-        low_gate.T,
-        low_up.T,
-        norm_gain.reshape(1, ROWS),
-        high_gate,
-        high_up,
+        6,
+        *(
+            pltpu.with_memory_space_constraint(a, pltpu.HBM)
+            for a in (
+                weight_gate,
+                weight_up,
+                low_gate.T,
+                low_up.T,
+                norm_gain.reshape(1, ROWS),
+                high_gate,
+                high_up,
+            )
+        ),
         specs=[hbm] * 7,
         scratch=[
             pltpu.VMEM((2, RANK, ROWS), jnp.bfloat16),
@@ -288,35 +290,32 @@
     for step in (1, -1):
         held[0, -step] = sent(block, SECOND[step])
 
-    sums = small(sums_kernel, a_sum, 6, block, high)
-    total = small(add_kernel, a_sum, 2, sums, sent(sums, SIDE))
-    for axis, along, bit in (("x", ALONG_X, 1), ("y", ALONG_Y, 3)):
+    total = small(sums_kernel, a_sum, 6, block, high)
+    for along, bits in ((SECOND, (3, 1)), (FIRST, (1, 3))):
         others = [sent(total, along[d]) for d in (1, -1, 2)]
-        total = small(
-            functools.partial(ring_kernel, bit),
-            a_sum if axis == "x" else (a_sum, a_sum),
-            2,
-            total,
-            *others,
-        )
-    factor, inv = total
-
-    top, bottom = small(
-        halves_kernel,
-        (shape((TOP, FULL), jnp.bfloat16), shape((ROWS - TOP, FULL), jnp.bfloat16)),
-        6,
-        held[-1, 0],
-        held[1, 0],
-    )
+        body = functools.partial(ring_kernel, bits)
+        total = small(body, a_sum, 2, total, *others)
+    twin = sent(total, SIDE)
+    factor, inv = small(factor_kernel, (a_sum, a_sum), 2, total, twin)
+
+    def halves(a, b):
+        shapes = (shape((TOP, FULL), jnp.bfloat16), shape((ROWS - TOP, FULL), jnp.bfloat16))
+        return small(halves_kernel, shapes, 6, a, b)
+
+    top, bottom = halves(held[-1, 0], held[1, 0])
     top, bottom = sent(top, FIRST[1]), sent(bottom, FIRST[-1])
     held[2, 0] = small(joined_kernel, a_block, 6, top, bottom)
 
     for step, order in ((1, (-1, 1, 2)), (-1, (1, -1, 2))):
         for f in order:
             held[f, -step] = sent(held[f, 0], SECOND[step])
-    for step, order in ((1, (0, -1)), (-1, (1, 2))):
-        for f in order:
-            held[f, 2] = sent(held[f, -step], SECOND[step])
+    held[0, 2] = sent(held[0, -1], SECOND[1])
+    held[1, 2] = sent(held[1, 1], SECOND[-1])
+    pieces = []
+    for step, f in ((1, -1), (-1, 2)):
+        block = held[f, -step]
+        top, bottom = halves(block, block)
+        pieces.append([sent(p, SECOND[step]) for p in (top, bottom)])
 
     pairs = (
         ((0, 0), (-1, 0)),
@@ -326,22 +325,20 @@
         ((1, -1), (-1, 1)),
         ((2, -1), (2, 1)),
         ((0, 2), (1, 2)),
-        ((-1, 2), (2, 2)),
     )
+    last = ((-1, 2), (2, 2))
+    work = [([held[p] for p in pair], pair, 0) for pair in pairs]
+    work += [(piece, last, start) for piece, start in zip(zip(*pieces), (0, TOP))]
+    late = {k: (k - 2,) for k in range(2, len(pairs))}
+    late[len(pairs)] = (len(pairs) - 2, len(pairs) - 1)
     outs, moved = None, []
-    for k, pair in enumerate(pairs):
-        late = k - 2
-        *outs, ready = merged(
-            [held[p] for p in pair],
-            pair,
-            pairs[late] if late >= 0 else (),
-            high,
-            inv,
-            [moved[late]] if late >= 0 else [],
-            outs,
-        )
+    for k, (blocks, pair, start) in enumerate(work):
+        theirs = [work[j][1:] for j in late.get(k, ())]
+        arrived = [moved[j] for j in late.get(k, ())]
+        *outs, ready = merged(blocks, pair, start, theirs, high, inv, arrived, outs)
         moved.append(sent(ready, SIDE))
-    ready_gate, ready_up = placed(pairs[-2:], moved[-2:], outs)
+    theirs = [work[j][1:] for j in (-2, -1)]
+    ready_gate, ready_up = placed(theirs, moved[-2:], outs)
     factor = factor.reshape(WIDE)
     return ready_gate, ready_up, factor[:HALF], factor[HALF:]
 

time: 140 us -> 131 us (0.936)
  waiting for transfers between devices: 68.7 us -> 59.2 us
  starting transfers between devices: 45.8 us -> 52 us
  local copies, waits for them, and re-layouts: 3.87 us -> 0.65 us
  Pallas kernels: 20.7 us -> 18.4 us
    ppermute x31 -> x34, waiting for transfers between devices: 68.7 us -> 59.2 us  [sent(): return lax.ppermute(array, 'shard', pairs)]
    ppermute x31 -> x34, starting transfers between devices: 45.8 us -> 52 us  [sent(): return lax.ppermute(array, 'shard', pairs)]
    unnamed x6 -> x0, local copies, waits for them, and re-layouts: 3.22 us -> none
    pallas_call x7 -> x9, Pallas kernels: 4.17 us -> 2.01 us  [small(): pl.pallas_call(body, out_shape=outs, in_specs=specs or in_vmem(len(operan...]
    pallas_call x8 -> x9, Pallas kernels: 14.8 us -> 15.2 us  [merged(): pl.pallas_call(body, out_shape=(OUT, OUT, jax.ShapeDtypeStruct((n, rows,...]
  transfers between devices with their start and end apart: 31 -> 34, of which waited for: 16 -> 16; matrix products, arithmetic and copies ran while one was open for 0% -> 0% of each run, Pallas kernels for 11% -> 11%
where the time goes in v2:
time: 131 us
  waiting for transfers between devices  59.2 us (45%)
  starting transfers between devices  52 us (40%)
  Pallas kernels  18.4 us (14%)
    ppermute x34, waiting for transfers between devices, sent(): return lax.ppermute(array, 'shard', pairs)  59.2 us
    ppermute x34, starting transfers between devices, sent(): return lax.ppermute(array, 'shard', pairs)  52 us
    pallas_call x9, Pallas kernels, merged(): pl.pallas_call(body, out_shape=(OUT, OUT, jax.ShapeDtypeStruct((n, rows,...  15.2 us
  transfers between devices with their start and end apart: 34, of which 16 were waited for; matrix products, arithmetic and copies ran while one was open for 0% of the time, Pallas kernels for 11%

profile of v2, /device:TPU:1, one launch (start us, length us, event | category | flops | bytes accessed | tf_op | source)
XLA Modules:
  0.0 131.3 jit_solution(3102699709491057780)
XLA Ops:
  0.6 1.3 shard_map.102
  1.9 2.2 %collective-permute-start = (bf16[80,4992]{1,0:T(8,128)(2,1)S(1)}, bf16[80,4992]{1,0:T(8,128)(2,1)S(1)}, u32[]{:S(2)}, u32[]{:S(2)}) collective-permute-start(bf16[80,4992]{1,0:T(8,128)(2,1)S(1)} %get-tuple-element.43.block.refs_0_), channel_id=1, source_target_pairs={{0,8},{4,36},{8,16},{12,44},{16,24},{20,52},{24,0},{28,60},{32,40}... | collective-permute-start | bytes 2396168 | tf_op jit(solution)/shard_map/ppermute | solution.py:50
  4.1 0.4 shard_map.107.own
  4.6 2.8 %collective-permute-start.10 = (f32[1,4864]{1,0:T(1,128)S(1)}, f32[1,4864]{1,0:T(1,128)S(1)}, u32[]{:S(2)}, u32[]{:S(2)}) collective-permute-start(f32[1,4864]{1,0:T(1,128)S(1)} %shard_map.107.own), channel_id=1, source_target_pairs={{0,64},{4,20},{8,72},{12,28},{16,80},{20,4},{24,88},{28,12},{32,96... | collective-permute-start | bytes 58376 | tf_op jit(solution)/shard_map/ppermute | solution.py:50
  7.4 0.3 collective-permute-start.8
  7.7 2.4 %collective-permute-start.9 = (f32[1,4864]{1,0:T(1,128)S(1)}, f32[1,4864]{1,0:T(1,128)S(1)}, u32[]{:S(2)}, u32[]{:S(2)}) collective-permute-start(f32[1,4864]{1,0:T(1,128)S(1)} %shard_map.107.own), channel_id=1, source_target_pairs={{0,96},{4,28},{8,104},{12,4},{16,112},{20,12},{24,120},{28,20},{32... | collective-permute-start | bytes 58376 | tf_op jit(solution)/shard_map/ppermute | solution.py:50
  10.1 0.0 collective-permute-done.10.far
  10.1 1.7 %collective-permute-done.8.plus = f32[1,4864]{1,0:T(1,128)S(1)} collective-permute-done((f32[1,4864]{1,0:T(1,128)S(1)}, f32[1,4864]{1,0:T(1,128)S(1)}, u32[]{:S(2)}, u32[]{:S(2)}) %collective-permute-start.8) | collective-permute-done | bytes 19488 | tf_op jit(solution)/shard_map/ppermute | solution.py:50
  11.7 0.0 collective-permute-done.9.minus
  11.8 1.4 %collective-permute-start.11 = (f32[1,4864]{1,0:T(1,128)S(1)}, f32[1,4864]{1,0:T(1,128)S(1)}, u32[]{:S(2)}, u32[]{:S(2)}) collective-permute-start(f32[1,4864]{1,0:T(1,128)S(1)} %shard_map.108.own), channel_id=1, source_target_pairs={{0,8},{4,36},{8,16},{12,44},{16,24},{20,52},{24,0},{28,60},{32,40}... | collective-permute-start | bytes 58376 | tf_op jit(solution)/shard_map/ppermute | solution.py:50
  13.1 1.4 %collective-permute-start.12 = (f32[1,4864]{1,0:T(1,128)S(1)}, f32[1,4864]{1,0:T(1,128)S(1)}, u32[]{:S(2)}, u32[]{:S(2)}) collective-permute-start(f32[1,4864]{1,0:T(1,128)S(1)} %shard_map.108.own), channel_id=1, source_target_pairs={{0,24},{4,100},{8,0},{12,108},{16,8},{20,116},{24,16},{28,124},{32... | collective-permute-start | bytes 58376 | tf_op jit(solution)/shard_map/ppermute | solution.py:50
  14.5 1.4 %collective-permute-start.13 = (f32[1,4864]{1,0:T(1,128)S(1)}, f32[1,4864]{1,0:T(1,128)S(1)}, u32[]{:S(2)}, u32[]{:S(2)}) collective-permute-start(f32[1,4864]{1,0:T(1,128)S(1)} %shard_map.108.own), channel_id=1, source_target_pairs={{0,16},{4,68},{8,24},{12,76},{16,0},{20,84},{24,8},{28,92},{32,48}... | collective-permute-start | bytes 58376 | tf_op jit(solution)/shard_map/ppermute | solution.py:50
  15.9 0.1 collective-permute-done.11.plus
  16.0 0.1 collective-permute-done.12.minus
  16.0 2.6 %collective-permute-done.13.far = f32[1,4864]{1,0:T(1,128)S(1)} collective-permute-done((f32[1,4864]{1,0:T(1,128)S(1)}, f32[1,4864]{1,0:T(1,128)S(1)}, u32[]{:S(2)}, u32[]{:S(2)}) %collective-permute-start.13) | collective-permute-done | bytes 19488 | tf_op jit(solution)/shard_map/ppermute | solution.py:50
  18.7 4.0 %collective-permute-start.14 = (f32[1,4864]{1,0:T(1,128)S(1)}, f32[1,4864]{1,0:T(1,128)S(1)}, u32[]{:S(2)}, u32[]{:S(2)}) collective-permute-start(f32[1,4864]{1,0:T(1,128)S(1)} %shard_map.109.mine), channel_id=1, source_target_pairs={{0,4},{4,0},{8,12},{12,8},{16,20},{20,16},{24,28},{28,24},{32,36},... | collective-permute-start | bytes 58376 | tf_op jit(solution)/shard_map/ppermute | solution.py:50
  22.6 0.8 collective-permute-done.14.theirs
  23.5 1.6 %shard_map.111 = (bf16[2560,2432]{1,0:T(8,128)(2,1)}, bf16[2560,2432]{1,0:T(8,128)(2,1)}, bf16[2,80,4864]{2,1,0:T(8,128)(2,1)S(1)}) custom-call(bf16[80,4992]{1,0:T(8,128)(2,1)S(1)} %get-tuple-element.43.block.refs_0_, bf16[80,4992]{1,0:T(8,128)(2,1)S(1)} %collective-permute-done.a.refs_1_, bf16[64,4864]{1,0:T(8,128)(2,1)S(1)} %get-tuple-element.48.high.refs_2_, ...), custom_call_target="tpu_custom_call" | custom-call | flops 6000000 | bytes 1 | tf_op jit(solution)/shard_map/pallas_call | solution.py:231
  25.1 0.4 collective-permute-start.20
  25.5 2.7 %collective-permute-start.3 = (bf16[80,4992]{1,0:T(8,128)(2,1)S(1)}, bf16[80,4992]{1,0:T(8,128)(2,1)S(1)}, u32[]{:S(2)}, u32[]{:S(2)}) collective-permute-start(bf16[80,4992]{1,0:T(8,128)(2,1)S(1)} %get-tuple-element.43.block.refs_0_), channel_id=1, source_target_pairs={{0,24},{4,100},{8,0},{12,108},{16,8},{20,116},{24,16},{28,124},{32... | collective-permute-start | bytes 2396168 | tf_op jit(solution)/shard_map/ppermute | solution.py:50
  28.3 0.0 collective-permute-start.17
  28.3 2.7 %collective-permute-start.18 = (bf16[80,4992]{1,0:T(8,128)(2,1)S(1)}, bf16[80,4992]{1,0:T(8,128)(2,1)S(1)}, u32[]{:S(2)}, u32[]{:S(2)}) collective-permute-start(bf16[80,4992]{1,0:T(8,128)(2,1)S(1)} %get-tuple-element.43.block.refs_0_), channel_id=1, source_target_pairs={{0,96},{4,28},{8,104},{12,4},{16,112},{20,12},{24,120},{28,20},{32... | collective-permute-start | bytes 2396168 | tf_op jit(solution)/shard_map/ppermute | solution.py:50
  30.9 13.6 %collective-permute-done.3.b.refs_0_ = bf16[80,4992]{1,0:T(8,128)(2,1)S(1)} collective-permute-done((bf16[80,4992]{1,0:T(8,128)(2,1)S(1)}, bf16[80,4992]{1,0:T(8,128)(2,1)S(1)}, u32[]{:S(2)}, u32[]{:S(2)}) %collective-permute-start.3) | collective-permute-done | bytes 798752 | tf_op jit(solution)/shard_map/ppermute | solution.py:50
  44.5 0.1 shard_map.104
  44.6 0.1 collective-permute-start.4
  44.7 3.5 %collective-permute-start.5 = (bf16[32,4992]{1,0:T(8,128)(2,1)S(1)}, bf16[32,4992]{1,0:T(8,128)(2,1)S(1)}, u32[]{:S(2)}, u32[]{:S(2)}) collective-permute-start(bf16[32,4992]{1,0:T(8,128)(2,1)S(1)} %get-tuple-element.46), channel_id=1, source_target_pairs={{0,24},{4,100},{8,0},{12,108},{16,8},{20,116},{24,16},{28,124},{32... | collective-permute-start | bytes 958472 | tf_op jit(solution)/shard_map/ppermute | solution.py:50
  48.1 1.6 %shard_map.112 = (bf16[2560,2432]{1,0:T(8,128)(2,1)}, bf16[2560,2432]{1,0:T(8,128)(2,1)}, bf16[2,80,4864]{2,1,0:T(8,128)(2,1)S(1)}) custom-call(bf16[80,4992]{1,0:T(8,128)(2,1)S(1)} %collective-permute-done.17.refs_0_, bf16[80,4992]{1,0:T(8,128)(2,1)S(1)} %collective-permute-done.18.refs_1_, ...), custom_call_target="tpu_custom_call", output_to_operand_aliasing={{0}: (4, {}), {1}: (5, {})} | custom-call | flops 6000000 | bytes 1 | tf_op jit(solution)/shard_map/pallas_call | solution.py:231
  49.8 0.1 collective-permute-start.19
  49.9 2.2 %collective-permute-done.5.bottom = bf16[32,4992]{1,0:T(8,128)(2,1)S(1)} collective-permute-done((bf16[32,4992]{1,0:T(8,128)(2,1)S(1)}, bf16[32,4992]{1,0:T(8,128)(2,1)S(1)}, u32[]{:S(2)}, u32[]{:S(2)}) %collective-permute-start.5) | collective-permute-done | bytes 319520 | tf_op jit(solution)/shard_map/ppermute | solution.py:50
  52.1 3.5 %collective-permute-done.4.top = bf16[48,4992]{1,0:T(8,128)(2,1)S(1)} collective-permute-done((bf16[48,4992]{1,0:T(8,128)(2,1)S(1)}, bf16[48,4992]{1,0:T(8,128)(2,1)S(1)}, u32[]{:S(2)}, u32[]{:S(2)}) %collective-permute-start.4) | collective-permute-done | bytes 479264 | tf_op jit(solution)/shard_map/ppermute | solution.py:50
  55.6 0.1 shard_map.105.refs_1_
  55.7 1.8 %shard_map.113 = (bf16[2560,2432]{1,0:T(8,128)(2,1)}, bf16[2560,2432]{1,0:T(8,128)(2,1)}, bf16[2,80,4864]{2,1,0:T(8,128)(2,1)S(1)}) custom-call(bf16[80,4992]{1,0:T(8,128)(2,1)S(1)} %collective-permute-done.3.b.refs_0_, bf16[80,4992]{1,0:T(8,128)(2,1)S(1)} %shard_map.105.refs_1_, ...), custom_call_target="tpu_custom_call", output_to_operand_aliasing={{0}: (5, {}), {1}: (6, {})} | custom-call | flops 6000000 | bytes 1 | tf_op jit(solution)/shard_map/pallas_call | solution.py:231
  57.4 0.6 collective-permute-start.24
  58.0 1.5 %collective-permute-start.22 = (bf16[80,4992]{1,0:T(8,128)(2,1)S(1)}, bf16[80,4992]{1,0:T(8,128)(2,1)S(1)}, u32[]{:S(2)}, u32[]{:S(2)}) collective-permute-start(bf16[80,4992]{1,0:T(8,128)(2,1)S(1)} %collective-permute-done.3.b.refs_0_), channel_id=1, source_target_pairs={{0,32},{4,12},{8,40},{12,20},{16,48},{20,28},{24,56},{28,4},{32,64... | collective-permute-start | bytes 2396168 | tf_op jit(solution)/shard_map/ppermute | solution.py:50
  59.5 3.0 %collective-permute-done.1.a.b.refs_0_ = bf16[80,4992]{1,0:T(8,128)(2,1)S(1)} collective-permute-done((bf16[80,4992]{1,0:T(8,128)(2,1)S(1)}, bf16[80,4992]{1,0:T(8,128)(2,1)S(1)}, u32[]{:S(2)}, u32[]{:S(2)}) %collective-permute-start.1) | collective-permute-done | bytes 798752 | tf_op jit(solution)/shard_map/ppermute | solution.py:50
  62.5 6.8 %collective-permute-done.16.refs_1_ = bf16[80,4992]{1,0:T(8,128)(2,1)S(1)} collective-permute-done((bf16[80,4992]{1,0:T(8,128)(2,1)S(1)}, bf16[80,4992]{1,0:T(8,128)(2,1)S(1)}, u32[]{:S(2)}, u32[]{:S(2)}) %collective-permute-start.16) | collective-permute-done | bytes 798752 | tf_op jit(solution)/shard_map/ppermute | solution.py:50
  69.3 1.2 collective-permute-start.6
  70.5 1.7 %shard_map.114 = (bf16[2560,2432]{1,0:T(8,128)(2,1)}, bf16[2560,2432]{1,0:T(8,128)(2,1)}, bf16[2,80,4864]{2,1,0:T(8,128)(2,1)S(1)}) custom-call(bf16[80,4992]{1,0:T(8,128)(2,1)S(1)} %collective-permute-done.1.a.b.refs_0_, bf16[80,4992]{1,0:T(8,128)(2,1)S(1)} %collective-permute-done.16.refs_1_, ...), custom_call_target="tpu_custom_call", output_to_operand_aliasing={{0}: (5, {}), {1}: (6, {})} | custom-call | flops 6000000 | bytes 1 | tf_op jit(solution)/shard_map/pallas_call | solution.py:231
  72.3 8.4 %collective-permute-start.21 = (bf16[2,80,4864]{2,1,0:T(8,128)(2,1)S(1)}, bf16[2,80,4864]{2,1,0:T(8,128)(2,1)S(1)}, u32[]{:S(2)}, u32[]{:S(2)}) collective-permute-start(bf16[2,80,4864]{2,1,0:T(8,128)(2,1)S(1)} %get-tuple-element.58), channel_id=1, source_target_pairs={{0,4},{4,0},{8,12},{12,8},{16,20},{20,16},{24,28},{28,24},{32,36},... | collective-permute-start | bytes 4669448 | tf_op jit(solution)/shard_map/ppermute | solution.py:50
  80.7 1.8 %shard_map.115 = (bf16[2560,2432]{1,0:T(8,128)(2,1)}, bf16[2560,2432]{1,0:T(8,128)(2,1)}, bf16[2,80,4864]{2,1,0:T(8,128)(2,1)S(1)}) custom-call(bf16[80,4992]{1,0:T(8,128)(2,1)S(1)} %collective-permute-done.22.refs_0_, bf16[80,4992]{1,0:T(8,128)(2,1)S(1)} %collective-permute-done.23.refs_1_, ...), custom_call_target="tpu_custom_call", output_to_operand_aliasing={{0}: (5, {}), {1}: (6, {})} | custom-call | flops 6000000 | bytes 1 | tf_op jit(solution)/shard_map/pallas_call | solution.py:231
  82.4 3.1 %collective-permute-start.28 = (bf16[2,80,4864]{2,1,0:T(8,128)(2,1)S(1)}, bf16[2,80,4864]{2,1,0:T(8,128)(2,1)S(1)}, u32[]{:S(2)}, u32[]{:S(2)}) collective-permute-start(bf16[2,80,4864]{2,1,0:T(8,128)(2,1)S(1)} %get-tuple-element.65), channel_id=1, source_target_pairs={{0,4},{4,0},{8,12},{12,8},{16,20},{20,16},{24,28},{28,24},{32,36},... | collective-permute-start | bytes 4669448 | tf_op jit(solution)/shard_map/ppermute | solution.py:50
  85.5 0.0 collective-permute-start.15
  85.5 0.2 collective-permute-start.26
  85.7 0.7 collective-permute-done.6.a.b.refs_1_
  86.4 1.8 %collective-permute-start.27 = (bf16[80,4992]{1,0:T(8,128)(2,1)S(1)}, bf16[80,4992]{1,0:T(8,128)(2,1)S(1)}, u32[]{:S(2)}, u32[]{:S(2)}) collective-permute-start(bf16[80,4992]{1,0:T(8,128)(2,1)S(1)} %collective-permute-done.16.refs_1_), channel_id=1, source_target_pairs={{0,96},{4,28},{8,104},{12,4},{16,112},{20,12},{24,120},{28,20},{32... | collective-permute-start | bytes 2396168 | tf_op jit(solution)/shard_map/ppermute | solution.py:50
  88.2 9.8 %collective-permute-done.15.refs_0_ = bf16[80,4992]{1,0:T(8,128)(2,1)S(1)} collective-permute-done((bf16[80,4992]{1,0:T(8,128)(2,1)S(1)}, bf16[80,4992]{1,0:T(8,128)(2,1)S(1)}, u32[]{:S(2)}, u32[]{:S(2)}) %collective-permute-start.15) | collective-permute-done | bytes 798752 | tf_op jit(solution)/shard_map/ppermute | solution.py:50
  98.0 1.8 %shard_map.116 = (bf16[2560,2432]{1,0:T(8,128)(2,1)}, bf16[2560,2432]{1,0:T(8,128)(2,1)}, bf16[2,80,4864]{2,1,0:T(8,128)(2,1)S(1)}) custom-call(bf16[80,4992]{1,0:T(8,128)(2,1)S(1)} %collective-permute-done.15.refs_0_, bf16[80,4992]{1,0:T(8,128)(2,1)S(1)} %collective-permute-done.6.a.b.refs_1_, ...), custom_call_target="tpu_custom_call", output_to_operand_aliasing={{0}: (5, {}), {1}: (6, {})} | custom-call | flops 6000000 | bytes 1 | tf_op jit(solution)/shard_map/pallas_call | solution.py:231
  99.8 1.7 %collective-permute-start.25 = (bf16[2,80,4864]{2,1,0:T(8,128)(2,1)S(1)}, bf16[2,80,4864]{2,1,0:T(8,128)(2,1)S(1)}, u32[]{:S(2)}, u32[]{:S(2)}) collective-permute-start(bf16[2,80,4864]{2,1,0:T(8,128)(2,1)S(1)} %get-tuple-element.64), channel_id=1, source_target_pairs={{0,4},{4,0},{8,12},{12,8},{16,20},{20,16},{24,28},{28,24},{32,36},... | collective-permute-start | bytes 4669448 | tf_op jit(solution)/shard_map/ppermute | solution.py:50
  101.4 5.1 %collective-permute-done.26.refs_0_ = bf16[80,4992]{1,0:T(8,128)(2,1)S(1)} collective-permute-done((bf16[80,4992]{1,0:T(8,128)(2,1)S(1)}, bf16[80,4992]{1,0:T(8,128)(2,1)S(1)}, u32[]{:S(2)}, u32[]{:S(2)}) %collective-permute-start.26) | collective-permute-done | bytes 798752 | tf_op jit(solution)/shard_map/ppermute | solution.py:50
  106.6 1.8 %shard_map.117 = (bf16[2560,2432]{1,0:T(8,128)(2,1)}, bf16[2560,2432]{1,0:T(8,128)(2,1)}, bf16[2,80,4864]{2,1,0:T(8,128)(2,1)S(1)}) custom-call(bf16[80,4992]{1,0:T(8,128)(2,1)S(1)} %collective-permute-done.26.refs_0_, bf16[80,4992]{1,0:T(8,128)(2,1)S(1)} %collective-permute-done.27.refs_1_, ...), custom_call_target="tpu_custom_call", output_to_operand_aliasing={{0}: (5, {}), {1}: (6, {})} | custom-call | flops 6000000 | bytes 1 | tf_op jit(solution)/shard_map/pallas_call | solution.py:231
  108.3 1.7 %collective-permute-start.29 = (bf16[2,80,4864]{2,1,0:T(8,128)(2,1)S(1)}, bf16[2,80,4864]{2,1,0:T(8,128)(2,1)S(1)}, u32[]{:S(2)}, u32[]{:S(2)}) collective-permute-start(bf16[2,80,4864]{2,1,0:T(8,128)(2,1)S(1)} %get-tuple-element.68), channel_id=1, source_target_pairs={{0,4},{4,0},{8,12},{12,8},{16,20},{20,16},{24,28},{28,24},{32,36},... | collective-permute-start | bytes 4669448 | tf_op jit(solution)/shard_map/ppermute | solution.py:50
  110.0 0.1 shard_map.103
  110.0 0.1 collective-permute-start.2
  110.1 0.1 shard_map.106
  110.2 2.7 %collective-permute-start.7 = (bf16[48,4992]{1,0:T(8,128)(2,1)S(1)}, bf16[48,4992]{1,0:T(8,128)(2,1)S(1)}, u32[]{:S(2)}, u32[]{:S(2)}) collective-permute-start(bf16[48,4992]{1,0:T(8,128)(2,1)S(1)} %get-tuple-element.47), channel_id=1, source_target_pairs={{0,96},{4,28},{8,104},{12,4},{16,112},{20,12},{24,120},{28,20},{32... | collective-permute-start | bytes 1437704 | tf_op jit(solution)/shard_map/ppermute | solution.py:50
  112.9 6.2 %collective-permute-done.2.refs_0_ = bf16[48,4992]{1,0:T(8,128)(2,1)S(1)} collective-permute-done((bf16[48,4992]{1,0:T(8,128)(2,1)S(1)}, bf16[48,4992]{1,0:T(8,128)(2,1)S(1)}, u32[]{:S(2)}, u32[]{:S(2)}) %collective-permute-start.2) | collective-permute-done | bytes 479264 | tf_op jit(solution)/shard_map/ppermute | solution.py:50
  119.2 2.1 %shard_map.118 = (bf16[2560,2432]{1,0:T(8,128)(2,1)}, bf16[2560,2432]{1,0:T(8,128)(2,1)}, bf16[2,48,4864]{2,1,0:T(8,128)(2,1)S(1)}) custom-call(bf16[48,4992]{1,0:T(8,128)(2,1)S(1)} %collective-permute-done.2.refs_0_, bf16[48,4992]{1,0:T(8,128)(2,1)S(1)} %collective-permute-done.7.refs_1_, ...), custom_call_target="tpu_custom_call", output_to_operand_aliasing={{0}: (6, {}), {1}: (7, {})} | custom-call | flops 6000000 | bytes 1 | tf_op jit(solution)/shard_map/pallas_call | solution.py:231
  121.3 2.0 %collective-permute-start.30 = (bf16[2,48,4864]{2,1,0:T(8,128)(2,1)S(1)}, bf16[2,48,4864]{2,1,0:T(8,128)(2,1)S(1)}, u32[]{:S(2)}, u32[]{:S(2)}) collective-permute-start(bf16[2,48,4864]{2,1,0:T(8,128)(2,1)S(1)} %get-tuple-element.71), channel_id=1, source_target_pairs={{0,4},{4,0},{8,12},{12,8},{16,20},{20,16},{24,28},{28,24},{32,36},... | collective-permute-start | bytes 2801672 | tf_op jit(solution)/shard_map/ppermute | solution.py:50
  123.3 2.0 %collective-permute-done.32.refs_1_ = bf16[32,4992]{1,0:T(8,128)(2,1)S(1)} collective-permute-done((bf16[32,4992]{1,0:T(8,128)(2,1)S(1)}, bf16[32,4992]{1,0:T(8,128)(2,1)S(1)}, u32[]{:S(2)}, u32[]{:S(2)}) %collective-permute-start.32) | collective-permute-done | bytes 319520 | tf_op jit(solution)/shard_map/ppermute | solution.py:50
  125.3 1.1 shard_map.119
  126.4 1.8 %collective-permute-start.33 = (bf16[2,32,4864]{2,1,0:T(8,128)(2,1)S(1)}, bf16[2,32,4864]{2,1,0:T(8,128)(2,1)S(1)}, u32[]{:S(2)}, u32[]{:S(2)}) collective-permute-start(bf16[2,32,4864]{2,1,0:T(8,128)(2,1)S(1)} %get-tuple-element.76), channel_id=1, source_target_pairs={{0,4},{4,0},{8,12},{12,8},{16,20},{20,16},{24,28},{28,24},{32,36},... | collective-permute-start | bytes 1867784 | tf_op jit(solution)/shard_map/ppermute | solution.py:50
  128.2 0.6 slice_reduce_fusion
  128.9 1.0 collective-permute-done.33.refs_1_
  129.9 1.2 shard_map.120
  (24 shorter events, 0.1 us)
Async XLA Ops:
  1.9 21.5 %collective-permute-start = (bf16[80,4992]{1,0:T(8,128)(2,1)S(1)}, bf16[80,4992]{1,0:T(8,128)(2,1)S(1)}, u32[]{:S(2)}, u32[]{:S(2)}) collective-permute-start(bf16[80,4992]{1,0:T(8,128)(2,1)S(1)} %get-tuple-element.43.block.refs_0_), channel_id=1, source_target_pairs={{0,8},{4,36},{8,16},{12,44},{16,24},{20,52},{24,0},{28,60},{32,40}... | collective-permute-start | bytes 2396168 | tf_op jit(solution)/shard_map/ppermute | solution.py:50
  4.6 5.5 %collective-permute-start.10 = (f32[1,4864]{1,0:T(1,128)S(1)}, f32[1,4864]{1,0:T(1,128)S(1)}, u32[]{:S(2)}, u32[]{:S(2)}) collective-permute-start(f32[1,4864]{1,0:T(1,128)S(1)} %shard_map.107.own), channel_id=1, source_target_pairs={{0,64},{4,20},{8,72},{12,28},{16,80},{20,4},{24,88},{28,12},{32,96... | collective-permute-start | bytes 58376 | tf_op jit(solution)/shard_map/ppermute | solution.py:50
  7.4 4.3 %collective-permute-start.8 = (f32[1,4864]{1,0:T(1,128)S(1)}, f32[1,4864]{1,0:T(1,128)S(1)}, u32[]{:S(2)}, u32[]{:S(2)}) collective-permute-start(f32[1,4864]{1,0:T(1,128)S(1)} %shard_map.107.own), channel_id=1, source_target_pairs={{0,32},{4,12},{8,40},{12,20},{16,48},{20,28},{24,56},{28,4},{32,64... | collective-permute-start | bytes 58376 | tf_op jit(solution)/shard_map/ppermute | solution.py:50
  7.7 4.0 %collective-permute-start.9 = (f32[1,4864]{1,0:T(1,128)S(1)}, f32[1,4864]{1,0:T(1,128)S(1)}, u32[]{:S(2)}, u32[]{:S(2)}) collective-permute-start(f32[1,4864]{1,0:T(1,128)S(1)} %shard_map.107.own), channel_id=1, source_target_pairs={{0,96},{4,28},{8,104},{12,4},{16,112},{20,12},{24,120},{28,20},{32... | collective-permute-start | bytes 58376 | tf_op jit(solution)/shard_map/ppermute | solution.py:50
  11.8 4.2 %collective-permute-start.11 = (f32[1,4864]{1,0:T(1,128)S(1)}, f32[1,4864]{1,0:T(1,128)S(1)}, u32[]{:S(2)}, u32[]{:S(2)}) collective-permute-start(f32[1,4864]{1,0:T(1,128)S(1)} %shard_map.108.own), channel_id=1, source_target_pairs={{0,8},{4,36},{8,16},{12,44},{16,24},{20,52},{24,0},{28,60},{32,40}... | collective-permute-start | bytes 58376 | tf_op jit(solution)/shard_map/ppermute | solution.py:50
  13.1 2.9 %collective-permute-start.12 = (f32[1,4864]{1,0:T(1,128)S(1)}, f32[1,4864]{1,0:T(1,128)S(1)}, u32[]{:S(2)}, u32[]{:S(2)}) collective-permute-start(f32[1,4864]{1,0:T(1,128)S(1)} %shard_map.108.own), channel_id=1, source_target_pairs={{0,24},{4,100},{8,0},{12,108},{16,8},{20,116},{24,16},{28,124},{32... | collective-permute-start | bytes 58376 | tf_op jit(solution)/shard_map/ppermute | solution.py:50
  14.5 4.1 %collective-permute-start.13 = (f32[1,4864]{1,0:T(1,128)S(1)}, f32[1,4864]{1,0:T(1,128)S(1)}, u32[]{:S(2)}, u32[]{:S(2)}) collective-permute-start(f32[1,4864]{1,0:T(1,128)S(1)} %shard_map.108.own), channel_id=1, source_target_pairs={{0,16},{4,68},{8,24},{12,76},{16,0},{20,84},{24,8},{28,92},{32,48}... | collective-permute-start | bytes 58376 | tf_op jit(solution)/shard_map/ppermute | solution.py:50
  18.7 4.8 %collective-permute-start.14 = (f32[1,4864]{1,0:T(1,128)S(1)}, f32[1,4864]{1,0:T(1,128)S(1)}, u32[]{:S(2)}, u32[]{:S(2)}) collective-permute-start(f32[1,4864]{1,0:T(1,128)S(1)} %shard_map.109.mine), channel_id=1, source_target_pairs={{0,4},{4,0},{8,12},{12,8},{16,20},{20,16},{24,28},{28,24},{32,36},... | collective-permute-start | bytes 58376 | tf_op jit(solution)/shard_map/ppermute | solution.py:50
  25.1 30.5 %collective-permute-start.20 = (bf16[2,80,4864]{2,1,0:T(8,128)(2,1)S(1)}, bf16[2,80,4864]{2,1,0:T(8,128)(2,1)S(1)}, u32[]{:S(2)}, u32[]{:S(2)}) collective-permute-start(bf16[2,80,4864]{2,1,0:T(8,128)(2,1)S(1)} %get-tuple-element.53), channel_id=1, source_target_pairs={{0,4},{4,0},{8,12},{12,8},{16,20},{20,16},{24,28},{28,24},{32,36},... | collective-permute-start | bytes 4669448 | tf_op jit(solution)/shard_map/ppermute | solution.py:50
  25.5 19.0 %collective-permute-start.3 = (bf16[80,4992]{1,0:T(8,128)(2,1)S(1)}, bf16[80,4992]{1,0:T(8,128)(2,1)S(1)}, u32[]{:S(2)}, u32[]{:S(2)}) collective-permute-start(bf16[80,4992]{1,0:T(8,128)(2,1)S(1)} %get-tuple-element.43.block.refs_0_), channel_id=1, source_target_pairs={{0,24},{4,100},{8,0},{12,108},{16,8},{20,116},{24,16},{28,124},{32... | collective-permute-start | bytes 2396168 | tf_op jit(solution)/shard_map/ppermute | solution.py:50
  28.3 19.9 %collective-permute-start.17 = (bf16[80,4992]{1,0:T(8,128)(2,1)S(1)}, bf16[80,4992]{1,0:T(8,128)(2,1)S(1)}, u32[]{:S(2)}, u32[]{:S(2)}) collective-permute-start(bf16[80,4992]{1,0:T(8,128)(2,1)S(1)} %get-tuple-element.43.block.refs_0_), channel_id=1, source_target_pairs={{0,32},{4,12},{8,40},{12,20},{16,48},{20,28},{24,56},{28,4},{32,64... | collective-permute-start | bytes 2396168 | tf_op jit(solution)/shard_map/ppermute | solution.py:50
  28.3 19.9 %collective-permute-start.18 = (bf16[80,4992]{1,0:T(8,128)(2,1)S(1)}, bf16[80,4992]{1,0:T(8,128)(2,1)S(1)}, u32[]{:S(2)}, u32[]{:S(2)}) collective-permute-start(bf16[80,4992]{1,0:T(8,128)(2,1)S(1)} %get-tuple-element.43.block.refs_0_), channel_id=1, source_target_pairs={{0,96},{4,28},{8,104},{12,4},{16,112},{20,12},{24,120},{28,20},{32... | collective-permute-start | bytes 2396168 | tf_op jit(solution)/shard_map/ppermute | solution.py:50
  44.6 11.0 %collective-permute-start.4 = (bf16[48,4992]{1,0:T(8,128)(2,1)S(1)}, bf16[48,4992]{1,0:T(8,128)(2,1)S(1)}, u32[]{:S(2)}, u32[]{:S(2)}) collective-permute-start(bf16[48,4992]{1,0:T(8,128)(2,1)S(1)} %get-tuple-element.45), channel_id=1, source_target_pairs={{0,8},{4,36},{8,16},{12,44},{16,24},{20,52},{24,0},{28,60},{32,40}... | collective-permute-start | bytes 1437704 | tf_op jit(solution)/shard_map/ppermute | solution.py:50
  44.7 7.4 %collective-permute-start.5 = (bf16[32,4992]{1,0:T(8,128)(2,1)S(1)}, bf16[32,4992]{1,0:T(8,128)(2,1)S(1)}, u32[]{:S(2)}, u32[]{:S(2)}) collective-permute-start(bf16[32,4992]{1,0:T(8,128)(2,1)S(1)} %get-tuple-element.46), channel_id=1, source_target_pairs={{0,24},{4,100},{8,0},{12,108},{16,8},{20,116},{24,16},{28,124},{32... | collective-permute-start | bytes 958472 | tf_op jit(solution)/shard_map/ppermute | solution.py:50
  48.1 14.3 %collective-permute-start.1 = (bf16[80,4992]{1,0:T(8,128)(2,1)S(1)}, bf16[80,4992]{1,0:T(8,128)(2,1)S(1)}, u32[]{:S(2)}, u32[]{:S(2)}) collective-permute-start(bf16[80,4992]{1,0:T(8,128)(2,1)S(1)} %collective-permute-done.a.refs_1_), channel_id=1, source_target_pairs={{0,32},{4,12},{8,40},{12,20},{16,48},{20,28},{24,56},{28,4},{32,64... | collective-permute-start | bytes 2396168 | tf_op jit(solution)/shard_map/ppermute | solution.py:50
  49.8 20.8 %collective-permute-start.19 = (bf16[2,80,4864]{2,1,0:T(8,128)(2,1)S(1)}, bf16[2,80,4864]{2,1,0:T(8,128)(2,1)S(1)}, u32[]{:S(2)}, u32[]{:S(2)}) collective-permute-start(bf16[2,80,4864]{2,1,0:T(8,128)(2,1)S(1)} %get-tuple-element.52), channel_id=1, source_target_pairs={{0,4},{4,0},{8,12},{12,8},{16,20},{20,16},{24,28},{28,24},{32,36},... | collective-permute-start | bytes 4669448 | tf_op jit(solution)/shard_map/ppermute | solution.py:50
  57.4 23.3 %collective-permute-start.24 = (bf16[2,80,4864]{2,1,0:T(8,128)(2,1)S(1)}, bf16[2,80,4864]{2,1,0:T(8,128)(2,1)S(1)}, u32[]{:S(2)}, u32[]{:S(2)}) collective-permute-start(bf16[2,80,4864]{2,1,0:T(8,128)(2,1)S(1)} %get-tuple-element.59), channel_id=1, source_target_pairs={{0,4},{4,0},{8,12},{12,8},{16,20},{20,16},{24,28},{28,24},{32,36},... | collective-permute-start | bytes 4669448 | tf_op jit(solution)/shard_map/ppermute | solution.py:50
  58.0 11.3 %collective-permute-start.16 = (bf16[80,4992]{1,0:T(8,128)(2,1)S(1)}, bf16[80,4992]{1,0:T(8,128)(2,1)S(1)}, u32[]{:S(2)}, u32[]{:S(2)}) collective-permute-start(bf16[80,4992]{1,0:T(8,128)(2,1)S(1)} %collective-permute-done.3.b.refs_0_), channel_id=1, source_target_pairs={{0,96},{4,28},{8,104},{12,4},{16,112},{20,12},{24,120},{28,20},{32... | collective-permute-start | bytes 2396168 | tf_op jit(solution)/shard_map/ppermute | solution.py:50
  58.0 22.6 %collective-permute-start.22 = (bf16[80,4992]{1,0:T(8,128)(2,1)S(1)}, bf16[80,4992]{1,0:T(8,128)(2,1)S(1)}, u32[]{:S(2)}, u32[]{:S(2)}) collective-permute-start(bf16[80,4992]{1,0:T(8,128)(2,1)S(1)} %collective-permute-done.3.b.refs_0_), channel_id=1, source_target_pairs={{0,32},{4,12},{8,40},{12,20},{16,48},{20,28},{24,56},{28,4},{32,64... | collective-permute-start | bytes 2396168 | tf_op jit(solution)/shard_map/ppermute | solution.py:50
  62.5 18.2 %collective-permute-start.23 = (bf16[80,4992]{1,0:T(8,128)(2,1)S(1)}, bf16[80,4992]{1,0:T(8,128)(2,1)S(1)}, u32[]{:S(2)}, u32[]{:S(2)}) collective-permute-start(bf16[80,4992]{1,0:T(8,128)(2,1)S(1)} %collective-permute-done.a.refs_1_), channel_id=1, source_target_pairs={{0,96},{4,28},{8,104},{12,4},{16,112},{20,12},{24,120},{28,20},{32... | collective-permute-start | bytes 2396168 | tf_op jit(solution)/shard_map/ppermute | solution.py:50
  69.3 17.1 %collective-permute-start.6 = (bf16[80,4992]{1,0:T(8,128)(2,1)S(1)}, bf16[80,4992]{1,0:T(8,128)(2,1)S(1)}, u32[]{:S(2)}, u32[]{:S(2)}) collective-permute-start(bf16[80,4992]{1,0:T(8,128)(2,1)S(1)} %shard_map.105.refs_1_), channel_id=1, source_target_pairs={{0,96},{4,28},{8,104},{12,4},{16,112},{20,12},{24,120},{28,20},{32... | collective-permute-start | bytes 2396168 | tf_op jit(solution)/shard_map/ppermute | solution.py:50
  72.3 25.7 %collective-permute-start.21 = (bf16[2,80,4864]{2,1,0:T(8,128)(2,1)S(1)}, bf16[2,80,4864]{2,1,0:T(8,128)(2,1)S(1)}, u32[]{:S(2)}, u32[]{:S(2)}) collective-permute-start(bf16[2,80,4864]{2,1,0:T(8,128)(2,1)S(1)} %get-tuple-element.58), channel_id=1, source_target_pairs={{0,4},{4,0},{8,12},{12,8},{16,20},{20,16},{24,28},{28,24},{32,36},... | collective-permute-start | bytes 4669448 | tf_op jit(solution)/shard_map/ppermute | solution.py:50
  82.4 24.1 %collective-permute-start.28 = (bf16[2,80,4864]{2,1,0:T(8,128)(2,1)S(1)}, bf16[2,80,4864]{2,1,0:T(8,128)(2,1)S(1)}, u32[]{:S(2)}, u32[]{:S(2)}) collective-permute-start(bf16[2,80,4864]{2,1,0:T(8,128)(2,1)S(1)} %get-tuple-element.65), channel_id=1, source_target_pairs={{0,4},{4,0},{8,12},{12,8},{16,20},{20,16},{24,28},{28,24},{32,36},... | collective-permute-start | bytes 4669448 | tf_op jit(solution)/shard_map/ppermute | solution.py:50
  85.5 12.5 %collective-permute-start.15 = (bf16[80,4992]{1,0:T(8,128)(2,1)S(1)}, bf16[80,4992]{1,0:T(8,128)(2,1)S(1)}, u32[]{:S(2)}, u32[]{:S(2)}) collective-permute-start(bf16[80,4992]{1,0:T(8,128)(2,1)S(1)} %shard_map.105.refs_1_), channel_id=1, source_target_pairs={{0,32},{4,12},{8,40},{12,20},{16,48},{20,28},{24,56},{28,4},{32,64... | collective-permute-start | bytes 2396168 | tf_op jit(solution)/shard_map/ppermute | solution.py:50
  85.5 21.0 %collective-permute-start.26 = (bf16[80,4992]{1,0:T(8,128)(2,1)S(1)}, bf16[80,4992]{1,0:T(8,128)(2,1)S(1)}, u32[]{:S(2)}, u32[]{:S(2)}) collective-permute-start(bf16[80,4992]{1,0:T(8,128)(2,1)S(1)} %collective-permute-done.17.refs_0_), channel_id=1, source_target_pairs={{0,32},{4,12},{8,40},{12,20},{16,48},{20,28},{24,56},{28,4},{32,64... | collective-permute-start | bytes 2396168 | tf_op jit(solution)/shard_map/ppermute | solution.py:50
  86.4 20.1 %collective-permute-start.27 = (bf16[80,4992]{1,0:T(8,128)(2,1)S(1)}, bf16[80,4992]{1,0:T(8,128)(2,1)S(1)}, u32[]{:S(2)}, u32[]{:S(2)}) collective-permute-start(bf16[80,4992]{1,0:T(8,128)(2,1)S(1)} %collective-permute-done.16.refs_1_), channel_id=1, source_target_pairs={{0,96},{4,28},{8,104},{12,4},{16,112},{20,12},{24,120},{28,20},{32... | collective-permute-start | bytes 2396168 | tf_op jit(solution)/shard_map/ppermute | solution.py:50
  99.8 19.4 %collective-permute-start.25 = (bf16[2,80,4864]{2,1,0:T(8,128)(2,1)S(1)}, bf16[2,80,4864]{2,1,0:T(8,128)(2,1)S(1)}, u32[]{:S(2)}, u32[]{:S(2)}) collective-permute-start(bf16[2,80,4864]{2,1,0:T(8,128)(2,1)S(1)} %get-tuple-element.64), channel_id=1, source_target_pairs={{0,4},{4,0},{8,12},{12,8},{16,20},{20,16},{24,28},{28,24},{32,36},... | collective-permute-start | bytes 4669448 | tf_op jit(solution)/shard_map/ppermute | solution.py:50
  108.3 10.9 %collective-permute-start.29 = (bf16[2,80,4864]{2,1,0:T(8,128)(2,1)S(1)}, bf16[2,80,4864]{2,1,0:T(8,128)(2,1)S(1)}, u32[]{:S(2)}, u32[]{:S(2)}) collective-permute-start(bf16[2,80,4864]{2,1,0:T(8,128)(2,1)S(1)} %get-tuple-element.68), channel_id=1, source_target_pairs={{0,4},{4,0},{8,12},{12,8},{16,20},{20,16},{24,28},{28,24},{32,36},... | collective-permute-start | bytes 4669448 | tf_op jit(solution)/shard_map/ppermute | solution.py:50
  110.0 9.1 %collective-permute-start.2 = (bf16[48,4992]{1,0:T(8,128)(2,1)S(1)}, bf16[48,4992]{1,0:T(8,128)(2,1)S(1)}, u32[]{:S(2)}, u32[]{:S(2)}) collective-permute-start(bf16[48,4992]{1,0:T(8,128)(2,1)S(1)} %get-tuple-element.44), channel_id=1, source_target_pairs={{0,32},{4,12},{8,40},{12,20},{16,48},{20,28},{24,56},{28,4},{32,64... | collective-permute-start | bytes 1437704 | tf_op jit(solution)/shard_map/ppermute | solution.py:50
  110.2 9.0 %collective-permute-start.7 = (bf16[48,4992]{1,0:T(8,128)(2,1)S(1)}, bf16[48,4992]{1,0:T(8,128)(2,1)S(1)}, u32[]{:S(2)}, u32[]{:S(2)}) collective-permute-start(bf16[48,4992]{1,0:T(8,128)(2,1)S(1)} %get-tuple-element.47), channel_id=1, source_target_pairs={{0,96},{4,28},{8,104},{12,4},{16,112},{20,12},{24,120},{28,20},{32... | collective-permute-start | bytes 1437704 | tf_op jit(solution)/shard_map/ppermute | solution.py:50
  112.9 10.4 %collective-permute-start.31 = (bf16[32,4992]{1,0:T(8,128)(2,1)S(1)}, bf16[32,4992]{1,0:T(8,128)(2,1)S(1)}, u32[]{:S(2)}, u32[]{:S(2)}) collective-permute-start(bf16[32,4992]{1,0:T(8,128)(2,1)S(1)} %get-tuple-element.72), channel_id=1, source_target_pairs={{0,32},{4,12},{8,40},{12,20},{16,48},{20,28},{24,56},{28,4},{32,64... | collective-permute-start | bytes 958472 | tf_op jit(solution)/shard_map/ppermute | solution.py:50
  119.2 6.1 %collective-permute-start.32 = (bf16[32,4992]{1,0:T(8,128)(2,1)S(1)}, bf16[32,4992]{1,0:T(8,128)(2,1)S(1)}, u32[]{:S(2)}, u32[]{:S(2)}) collective-permute-start(bf16[32,4992]{1,0:T(8,128)(2,1)S(1)} %get-tuple-element.73), channel_id=1, source_target_pairs={{0,96},{4,28},{8,104},{12,4},{16,112},{20,12},{24,120},{28,20},{32... | collective-permute-start | bytes 958472 | tf_op jit(solution)/shard_map/ppermute | solution.py:50
  121.3 8.6 %collective-permute-start.30 = (bf16[2,48,4864]{2,1,0:T(8,128)(2,1)S(1)}, bf16[2,48,4864]{2,1,0:T(8,128)(2,1)S(1)}, u32[]{:S(2)}, u32[]{:S(2)}) collective-permute-start(bf16[2,48,4864]{2,1,0:T(8,128)(2,1)S(1)} %get-tuple-element.71), channel_id=1, source_target_pairs={{0,4},{4,0},{8,12},{12,8},{16,20},{20,16},{24,28},{28,24},{32,36},... | collective-permute-start | bytes 2801672 | tf_op jit(solution)/shard_map/ppermute | solution.py:50
  126.4 3.5 %collective-permute-start.33 = (bf16[2,32,4864]{2,1,0:T(8,128)(2,1)S(1)}, bf16[2,32,4864]{2,1,0:T(8,128)(2,1)S(1)}, u32[]{:S(2)}, u32[]{:S(2)}) collective-permute-start(bf16[2,32,4864]{2,1,0:T(8,128)(2,1)S(1)} %get-tuple-element.76), channel_id=1, source_target_pairs={{0,4},{4,0},{8,12},{12,8},{16,20},{20,16},{24,28},{28,24},{32,36},... | collective-permute-start | bytes 1867784 | tf_op jit(solution)/shard_map/ppermute | solution.py:50

commit v3 on v2

--- a/solution.py
+++ b/solution.py
@@ -15,6 +15,7 @@
 TILE = 256
 KIB = 1024
 RANK = 32
+CUT = 2560
 TOP = 48
 mix_rate = 2.0
 
@@ -119,14 +120,19 @@
     inv[...] = 1.0 / root
 
 
-def halves_kernel(a, b, top, bottom):
-    top[...] = a[:TOP]
-    bottom[...] = b[TOP:]
-
-
-def joined_kernel(top, bottom, block):
-    block[:TOP] = top[...]
-    block[TOP:] = bottom[...]
+def halves_kernel(a, b, left, right):
+    left[...] = a[:, :CUT]
+    right[...] = b[:, CUT:]
+
+
+def joined_kernel(left, right, block):
+    block[:, :CUT] = left[...]
+    block[:, CUT:] = right[...]
+
+
+def pieces_kernel(block, top, bottom):
+    top[...] = block[:TOP]
+    bottom[...] = block[TOP:]
 
 
 def placer(outs, sems, copies):
@@ -144,7 +150,7 @@
     return send
 
 
-def merge_kernel(mine, start, theirs, *refs):
+def merge_kernel(mine, start, flip, theirs, *refs):
     n, place = len(mine), len(theirs)
     blocks, refs = refs[:n], refs[n:]
     high, inv = refs[0], refs[1]
@@ -169,21 +175,9 @@
             ready[k, :, cols] = (v * gain[rows] * scale).astype(jnp.bfloat16)
         if j == HALF // TILE:
             for k in range(n):
-                send(ready.at[k], mine[k], start, 0, 0)
+                send(ready.at[k], mine[k], start, flip, 0)
     for k in range(n):
-        send(ready.at[k], mine[k], start, 0, 1)
-    for copy in copies:
-        copy.wait()
-
-
-def place_kernel(theirs, *refs):
-    moved, refs = refs[: len(theirs)], refs[len(theirs) + 2 :]
-    copies = []
-    send = placer(refs[:2], refs[2], copies)
-    for (pair, first), ref in zip(theirs, moved):
-        for k, at in enumerate(pair):
-            for h in range(2):
-                send(ref.at[k], at, first, 1, h)
+        send(ready.at[k], mine[k], start, flip, 1)
     for copy in copies:
         copy.wait()
 
@@ -212,7 +206,7 @@
     )(*operands)
 
 
-def merged(blocks, mine, start, theirs, high, inv, moved, outs):
+def merged(blocks, mine, start, flip, theirs, high, inv, moved, outs, hand_over):
     operands = [*blocks, high, inv, *moved]
     count = len(operands)
     aliases = {}
@@ -221,38 +215,26 @@
         outs = ()
 
         def body(*refs):
-            merge_kernel(mine, start, theirs, *refs[:count], None, None, *refs[count:])
+            merge_kernel(mine, start, flip, theirs, *refs[:count], None, None, *refs[count:])
     else:
         aliases = {count: 0, count + 1: 1}
         specs = specs + [ANY, ANY]
-        body = functools.partial(merge_kernel, mine, start, theirs)
+        body = functools.partial(merge_kernel, mine, start, flip, theirs)
     n, rows = len(mine), blocks[0].shape[0]
+    ready = (n, rows, WIDE)
+    kept = () if hand_over else (pltpu.VMEM(ready, jnp.bfloat16),)
+    given = (jax.ShapeDtypeStruct(ready, jnp.bfloat16),) if hand_over else ()
     copies = 2 * (n + sum(len(pair) for pair, _ in theirs))
     return pl.pallas_call(
         body,
-        out_shape=(OUT, OUT, jax.ShapeDtypeStruct((n, rows, WIDE), jnp.bfloat16)),
+        out_shape=(OUT, OUT, *given),
         in_specs=specs,
-        out_specs=(ANY, ANY, pl.BlockSpec(memory_space=pltpu.VMEM)),
-        scratch_shapes=[pltpu.SemaphoreType.DMA((copies,))],
+        out_specs=(ANY, ANY, *in_vmem(len(given))),
+        scratch_shapes=[*kept, pltpu.SemaphoreType.DMA((copies,))],
         input_output_aliases=aliases,
         compiler_params=params(14),
         cost_estimate=cost(1.5),
     )(*operands, *outs)
-
-
-def placed(theirs, moved, outs):
-    n = len(moved)
-    copies = 2 * sum(len(pair) for pair, _ in theirs)
-    return pl.pallas_call(
-        functools.partial(place_kernel, theirs),
-        out_shape=(OUT, OUT),
-        in_specs=in_vmem(n) + [ANY, ANY],
-        out_specs=(ANY, ANY),
-        scratch_shapes=[pltpu.SemaphoreType.DMA((copies,))],
-        input_output_aliases={n: 0, n + 1: 1},
-        compiler_params=params(10),
-        cost_estimate=cost(1.0),
-    )(*moved, *outs)
 
 
 def program(weight_gate, low_gate, high_gate, weight_up, low_up, high_up, norm_gain):
@@ -298,24 +280,28 @@
     twin = sent(total, SIDE)
     factor, inv = small(factor_kernel, (a_sum, a_sum), 2, total, twin)
 
-    def halves(a, b):
-        shapes = (shape((TOP, FULL), jnp.bfloat16), shape((ROWS - TOP, FULL), jnp.bfloat16))
-        return small(halves_kernel, shapes, 6, a, b)
-
-    top, bottom = halves(held[-1, 0], held[1, 0])
-    top, bottom = sent(top, FIRST[1]), sent(bottom, FIRST[-1])
-    held[2, 0] = small(joined_kernel, a_block, 6, top, bottom)
+    left, right = small(
+        halves_kernel,
+        (shape((ROWS, CUT), jnp.bfloat16), shape((ROWS, FULL - CUT), jnp.bfloat16)),
+        6,
+        held[-1, 0],
+        held[1, 0],
+    )
+    left, right = sent(left, FIRST[1]), sent(right, FIRST[-1])
+    held[2, 0] = small(joined_kernel, a_block, 6, left, right)
 
     for step, order in ((1, (-1, 1, 2)), (-1, (1, -1, 2))):
         for f in order:
             held[f, -step] = sent(held[f, 0], SECOND[step])
     held[0, 2] = sent(held[0, -1], SECOND[1])
     held[1, 2] = sent(held[1, 1], SECOND[-1])
-    pieces = []
+    tops, bottoms = [], []
+    shapes = (shape((TOP, FULL), jnp.bfloat16), shape((ROWS - TOP, FULL), jnp.bfloat16))
     for step, f in ((1, -1), (-1, 2)):
-        block = held[f, -step]
-        top, bottom = halves(block, block)
-        pieces.append([sent(p, SECOND[step]) for p in (top, bottom)])
+        top, bottom = small(pieces_kernel, shapes, 6, held[f, -step])
+        tops.append(sent(top, SECOND[step]))
+        bottoms.append(sent(bottom, SECOND[step]))
+    twins = [sent(bottom, SIDE) for bottom in bottoms]
 
     pairs = (
         ((0, 0), (-1, 0)),
@@ -327,18 +313,19 @@
         ((0, 2), (1, 2)),
     )
     last = ((-1, 2), (2, 2))
-    work = [([held[p] for p in pair], pair, 0) for pair in pairs]
-    work += [(piece, last, start) for piece, start in zip(zip(*pieces), (0, TOP))]
-    late = {k: (k - 2,) for k in range(2, len(pairs))}
-    late[len(pairs)] = (len(pairs) - 2, len(pairs) - 1)
+    work = [([held[p] for p in pair], pair, 0, 0) for pair in pairs]
+    work += [(tops, last, 0, 0), (bottoms, last, TOP, 0), (twins, last, TOP, 1)]
+    late = {k: (k - 2,) for k in range(2, 7)} | {7: (5, 6), 9: (7,)}
     outs, moved = None, []
-    for k, (blocks, pair, start) in enumerate(work):
-        theirs = [work[j][1:] for j in late.get(k, ())]
+    for k, (blocks, pair, start, flip) in enumerate(work):
+        theirs = [work[j][1:3] for j in late.get(k, ())]
         arrived = [moved[j] for j in late.get(k, ())]
-        *outs, ready = merged(blocks, pair, start, theirs, high, inv, arrived, outs)
-        moved.append(sent(ready, SIDE))
-    theirs = [work[j][1:] for j in (-2, -1)]
-    ready_gate, ready_up = placed(theirs, moved[-2:], outs)
+        hand_over = k < 8
+        results = merged(blocks, pair, start, flip, theirs, high, inv, arrived, outs, hand_over)
+        outs = results[:2]
+        if hand_over:
+            moved.append(sent(results[2], SIDE))
+    ready_gate, ready_up = outs
     factor = factor.reshape(WIDE)
     return ready_gate, ready_up, factor[:HALF], factor[HALF:]
 

time: 131 us -> 133 us (1.015)
  waiting for transfers between devices: 59.2 us -> 61 us
    ppermute x34 -> x35, waiting for transfers between devices: 59.2 us -> 61 us  [sent(): return lax.ppermute(array, 'shard', pairs)]
    ppermute x34 -> x35, starting transfers between devices: 52 us -> 51.2 us  [sent(): return lax.ppermute(array, 'shard', pairs)]
  transfers between devices with their start and end apart: 34 -> 35, of which waited for: 16 -> 16; matrix products, arithmetic and copies ran while one was open for 0% -> 0% of each run, Pallas kernels for 11% -> 9%
where the time goes in v3:
time: 133 us; the launch traced here: 132 us
  waiting for transfers between devices  61 us (46%)
  starting transfers between devices  51.2 us (38%)
  Pallas kernels  18.5 us (14%)
    ppermute x35, waiting for transfers between devices, sent(): return lax.ppermute(array, 'shard', pairs)  61 us
    ppermute x35, starting transfers between devices, sent(): return lax.ppermute(array, 'shard', pairs)  51.2 us
    pallas_call x10, Pallas kernels, merged(): pl.pallas_call(body, out_shape=(OUT, OUT, *given), in_specs=specs, out_sp...  16.5 us
  transfers between devices with their start and end apart: 35, of which 16 were waited for; matrix products, arithmetic and copies ran while one was open for 0% of the time, Pallas kernels for 9%

profile of v3, /device:TPU:1, one launch (start us, length us, event | category | flops | bytes accessed | tf_op | source)
XLA Modules:
  0.0 132.4 jit_solution(8164270114726598791)
XLA Ops:
  0.6 1.3 shard_map.102
  1.9 2.2 %collective-permute-start = (bf16[80,4992]{1,0:T(8,128)(2,1)S(1)}, bf16[80,4992]{1,0:T(8,128)(2,1)S(1)}, u32[]{:S(2)}, u32[]{:S(2)}) collective-permute-start(bf16[80,4992]{1,0:T(8,128)(2,1)S(1)} %get-tuple-element.42.block.refs_0_), channel_id=1, source_target_pairs={{0,8},{4,36},{8,16},{12,44},{16,24},{20,52},{24,0},{28,60},{32,40}... | collective-permute-start | bytes 2396168 | tf_op jit(solution)/shard_map/ppermute | solution.py:51
  4.1 0.4 shard_map.107.own
  4.6 1.3 collective-permute-start.10
  5.9 1.5 %collective-permute-start.11 = (f32[1,4864]{1,0:T(1,128)S(1)}, f32[1,4864]{1,0:T(1,128)S(1)}, u32[]{:S(2)}, u32[]{:S(2)}) collective-permute-start(f32[1,4864]{1,0:T(1,128)S(1)} %shard_map.107.own), channel_id=1, source_target_pairs={{0,96},{4,28},{8,104},{12,4},{16,112},{20,12},{24,120},{28,20},{32... | collective-permute-start | bytes 58376 | tf_op jit(solution)/shard_map/ppermute | solution.py:51
  7.3 1.5 %collective-permute-start.12 = (f32[1,4864]{1,0:T(1,128)S(1)}, f32[1,4864]{1,0:T(1,128)S(1)}, u32[]{:S(2)}, u32[]{:S(2)}) collective-permute-start(f32[1,4864]{1,0:T(1,128)S(1)} %shard_map.107.own), channel_id=1, source_target_pairs={{0,64},{4,20},{8,72},{12,28},{16,80},{20,4},{24,88},{28,12},{32,96... | collective-permute-start | bytes 58376 | tf_op jit(solution)/shard_map/ppermute | solution.py:51
  8.9 0.1 collective-permute-done.10.plus
  9.0 2.7 %collective-permute-done.12.far = f32[1,4864]{1,0:T(1,128)S(1)} collective-permute-done((f32[1,4864]{1,0:T(1,128)S(1)}, f32[1,4864]{1,0:T(1,128)S(1)}, u32[]{:S(2)}, u32[]{:S(2)}) %collective-permute-start.12) | collective-permute-done | bytes 19488 | tf_op jit(solution)/shard_map/ppermute | solution.py:51
  11.7 1.4 %collective-permute-start.13 = (f32[1,4864]{1,0:T(1,128)S(1)}, f32[1,4864]{1,0:T(1,128)S(1)}, u32[]{:S(2)}, u32[]{:S(2)}) collective-permute-start(f32[1,4864]{1,0:T(1,128)S(1)} %shard_map.108.own), channel_id=1, source_target_pairs={{0,8},{4,36},{8,16},{12,44},{16,24},{20,52},{24,0},{28,60},{32,40}... | collective-permute-start | bytes 58376 | tf_op jit(solution)/shard_map/ppermute | solution.py:51
  13.0 1.4 %collective-permute-start.14 = (f32[1,4864]{1,0:T(1,128)S(1)}, f32[1,4864]{1,0:T(1,128)S(1)}, u32[]{:S(2)}, u32[]{:S(2)}) collective-permute-start(f32[1,4864]{1,0:T(1,128)S(1)} %shard_map.108.own), channel_id=1, source_target_pairs={{0,24},{4,100},{8,0},{12,108},{16,8},{20,116},{24,16},{28,124},{32... | collective-permute-start | bytes 58376 | tf_op jit(solution)/shard_map/ppermute | solution.py:51
  14.4 1.4 %collective-permute-start.15 = (f32[1,4864]{1,0:T(1,128)S(1)}, f32[1,4864]{1,0:T(1,128)S(1)}, u32[]{:S(2)}, u32[]{:S(2)}) collective-permute-start(f32[1,4864]{1,0:T(1,128)S(1)} %shard_map.108.own), channel_id=1, source_target_pairs={{0,16},{4,68},{8,24},{12,76},{16,0},{20,84},{24,8},{28,92},{32,48}... | collective-permute-start | bytes 58376 | tf_op jit(solution)/shard_map/ppermute | solution.py:51
  15.8 0.2 collective-permute-done.13.plus
  16.0 2.5 %collective-permute-done.15.far = f32[1,4864]{1,0:T(1,128)S(1)} collective-permute-done((f32[1,4864]{1,0:T(1,128)S(1)}, f32[1,4864]{1,0:T(1,128)S(1)}, u32[]{:S(2)}, u32[]{:S(2)}) %collective-permute-start.15) | collective-permute-done | bytes 19488 | tf_op jit(solution)/shard_map/ppermute | solution.py:51
  18.6 4.4 %collective-permute-start.16 = (f32[1,4864]{1,0:T(1,128)S(1)}, f32[1,4864]{1,0:T(1,128)S(1)}, u32[]{:S(2)}, u32[]{:S(2)}) collective-permute-start(f32[1,4864]{1,0:T(1,128)S(1)} %shard_map.109.mine), channel_id=1, source_target_pairs={{0,4},{4,0},{8,12},{12,8},{16,20},{20,16},{24,28},{28,24},{32,36},... | collective-permute-start | bytes 58376 | tf_op jit(solution)/shard_map/ppermute | solution.py:51
  22.9 0.8 collective-permute-done.16.theirs
  23.8 0.0 collective-permute-done.a.refs_1_
  23.8 1.6 %shard_map.111 = (bf16[2560,2432]{1,0:T(8,128)(2,1)}, bf16[2560,2432]{1,0:T(8,128)(2,1)}, bf16[2,80,4864]{2,1,0:T(8,128)(2,1)S(1)}) custom-call(bf16[80,4992]{1,0:T(8,128)(2,1)S(1)} %get-tuple-element.42.block.refs_0_, bf16[80,4992]{1,0:T(8,128)(2,1)S(1)} %collective-permute-done.a.refs_1_, bf16[64,4864]{1,0:T(8,128)(2,1)S(1)} %get-tuple-element.47.high.refs_2_, ...), custom_call_target="tpu_custom_call" | custom-call | flops 6000000 | bytes 1 | tf_op jit(solution)/shard_map/pallas_call | solution.py:228
  25.4 0.4 collective-permute-start.24
  25.8 1.3 collective-permute-start.4
  27.2 2.7 %collective-permute-start.22 = (bf16[80,4992]{1,0:T(8,128)(2,1)S(1)}, bf16[80,4992]{1,0:T(8,128)(2,1)S(1)}, u32[]{:S(2)}, u32[]{:S(2)}) collective-permute-start(bf16[80,4992]{1,0:T(8,128)(2,1)S(1)} %get-tuple-element.42.block.refs_0_), channel_id=1, source_target_pairs={{0,96},{4,28},{8,104},{12,4},{16,112},{20,12},{24,120},{28,20},{32... | collective-permute-start | bytes 2396168 | tf_op jit(solution)/shard_map/ppermute | solution.py:51
  29.8 14.5 %collective-permute-done.4.b.refs_0_ = bf16[80,4992]{1,0:T(8,128)(2,1)S(1)} collective-permute-done((bf16[80,4992]{1,0:T(8,128)(2,1)S(1)}, bf16[80,4992]{1,0:T(8,128)(2,1)S(1)}, u32[]{:S(2)}, u32[]{:S(2)}) %collective-permute-start.4) | collective-permute-done | bytes 798752 | tf_op jit(solution)/shard_map/ppermute | solution.py:51
  44.3 0.1 shard_map.104
  44.4 0.1 collective-permute-start.5
  44.5 2.7 %collective-permute-start.6 = (bf16[80,2432]{1,0:T(8,128)(2,1)S(1)}, bf16[80,2432]{1,0:T(8,128)(2,1)S(1)}, u32[]{:S(2)}, u32[]{:S(2)}) collective-permute-start(bf16[80,2432]{1,0:T(8,128)(2,1)S(1)} %get-tuple-element.45), channel_id=1, source_target_pairs={{0,24},{4,100},{8,0},{12,108},{16,8},{20,116},{24,16},{28,124},{32... | collective-permute-start | bytes 1167368 | tf_op jit(solution)/shard_map/ppermute | solution.py:51
  47.2 1.6 %shard_map.112 = (bf16[2560,2432]{1,0:T(8,128)(2,1)}, bf16[2560,2432]{1,0:T(8,128)(2,1)}, bf16[2,80,4864]{2,1,0:T(8,128)(2,1)S(1)}) custom-call(bf16[80,4992]{1,0:T(8,128)(2,1)S(1)} %collective-permute-done.21.refs_0_, bf16[80,4992]{1,0:T(8,128)(2,1)S(1)} %collective-permute-done.22.refs_1_, ...), custom_call_target="tpu_custom_call", output_to_operand_aliasing={{0}: (4, {}), {1}: (5, {})} | custom-call | flops 6000000 | bytes 1 | tf_op jit(solution)/shard_map/pallas_call | solution.py:228
  48.8 2.3 %collective-permute-start.23 = (bf16[2,80,4864]{2,1,0:T(8,128)(2,1)S(1)}, bf16[2,80,4864]{2,1,0:T(8,128)(2,1)S(1)}, u32[]{:S(2)}, u32[]{:S(2)}) collective-permute-start(bf16[2,80,4864]{2,1,0:T(8,128)(2,1)S(1)} %get-tuple-element.53), channel_id=1, source_target_pairs={{0,4},{4,0},{8,12},{12,8},{16,20},{20,16},{24,28},{28,24},{32,36},... | collective-permute-start | bytes 4669448 | tf_op jit(solution)/shard_map/ppermute | solution.py:51
  51.1 0.8 collective-permute-done.6.right
  51.8 1.0 collective-permute-done.5.left
  52.8 0.1 shard_map.105.refs_1_
  52.8 1.8 %shard_map.113 = (bf16[2560,2432]{1,0:T(8,128)(2,1)}, bf16[2560,2432]{1,0:T(8,128)(2,1)}, bf16[2,80,4864]{2,1,0:T(8,128)(2,1)S(1)}) custom-call(bf16[80,4992]{1,0:T(8,128)(2,1)S(1)} %collective-permute-done.4.b.refs_0_, bf16[80,4992]{1,0:T(8,128)(2,1)S(1)} %shard_map.105.refs_1_, ...), custom_call_target="tpu_custom_call", output_to_operand_aliasing={{0}: (5, {}), {1}: (6, {})} | custom-call | flops 6000000 | bytes 1 | tf_op jit(solution)/shard_map/pallas_call | solution.py:228
  54.6 6.4 %collective-permute-start.28 = (bf16[2,80,4864]{2,1,0:T(8,128)(2,1)S(1)}, bf16[2,80,4864]{2,1,0:T(8,128)(2,1)S(1)}, u32[]{:S(2)}, u32[]{:S(2)}) collective-permute-start(bf16[2,80,4864]{2,1,0:T(8,128)(2,1)S(1)} %get-tuple-element.60), channel_id=1, source_target_pairs={{0,4},{4,0},{8,12},{12,8},{16,20},{20,16},{24,28},{28,24},{32,36},... | collective-permute-start | bytes 4669448 | tf_op jit(solution)/shard_map/ppermute | solution.py:51
  61.0 1.5 %collective-permute-start.26 = (bf16[80,4992]{1,0:T(8,128)(2,1)S(1)}, bf16[80,4992]{1,0:T(8,128)(2,1)S(1)}, u32[]{:S(2)}, u32[]{:S(2)}) collective-permute-start(bf16[80,4992]{1,0:T(8,128)(2,1)S(1)} %collective-permute-done.4.b.refs_0_), channel_id=1, source_target_pairs={{0,32},{4,12},{8,40},{12,20},{16,48},{20,28},{24,56},{28,4},{32,64... | collective-permute-start | bytes 2396168 | tf_op jit(solution)/shard_map/ppermute | solution.py:51
  62.4 0.7 collective-permute-done.1.block.refs_0_
  63.1 0.5 collective-permute-start.27
  63.7 8.6 %collective-permute-done.20.refs_1_ = bf16[80,4992]{1,0:T(8,128)(2,1)S(1)} collective-permute-done((bf16[80,4992]{1,0:T(8,128)(2,1)S(1)}, bf16[80,4992]{1,0:T(8,128)(2,1)S(1)}, u32[]{:S(2)}, u32[]{:S(2)}) %collective-permute-start.20) | collective-permute-done | bytes 798752 | tf_op jit(solution)/shard_map/ppermute | solution.py:51
  72.2 1.2 collective-permute-start.7
  73.5 1.7 %shard_map.114 = (bf16[2560,2432]{1,0:T(8,128)(2,1)}, bf16[2560,2432]{1,0:T(8,128)(2,1)}, bf16[2,80,4864]{2,1,0:T(8,128)(2,1)S(1)}) custom-call(bf16[80,4992]{1,0:T(8,128)(2,1)S(1)} %collective-permute-done.1.block.refs_0_, bf16[80,4992]{1,0:T(8,128)(2,1)S(1)} %collective-permute-done.20.refs_1_, ...), custom_call_target="tpu_custom_call", output_to_operand_aliasing={{0}: (5, {}), {1}: (6, {})} | custom-call | flops 6000000 | bytes 1 | tf_op jit(solution)/shard_map/pallas_call | solution.py:228
  75.2 3.8 %collective-permute-start.25 = (bf16[2,80,4864]{2,1,0:T(8,128)(2,1)S(1)}, bf16[2,80,4864]{2,1,0:T(8,128)(2,1)S(1)}, u32[]{:S(2)}, u32[]{:S(2)}) collective-permute-start(bf16[2,80,4864]{2,1,0:T(8,128)(2,1)S(1)} %get-tuple-element.59), channel_id=1, source_target_pairs={{0,4},{4,0},{8,12},{12,8},{16,20},{20,16},{24,28},{28,24},{32,36},... | collective-permute-start | bytes 4669448 | tf_op jit(solution)/shard_map/ppermute | solution.py:51
  79.1 1.7 %collective-permute-done.27.refs_1_ = bf16[80,4992]{1,0:T(8,128)(2,1)S(1)} collective-permute-done((bf16[80,4992]{1,0:T(8,128)(2,1)S(1)}, bf16[80,4992]{1,0:T(8,128)(2,1)S(1)}, u32[]{:S(2)}, u32[]{:S(2)}) %collective-permute-start.27) | collective-permute-done | bytes 798752 | tf_op jit(solution)/shard_map/ppermute | solution.py:51
  80.8 1.8 %shard_map.115 = (bf16[2560,2432]{1,0:T(8,128)(2,1)}, bf16[2560,2432]{1,0:T(8,128)(2,1)}, bf16[2,80,4864]{2,1,0:T(8,128)(2,1)S(1)}) custom-call(bf16[80,4992]{1,0:T(8,128)(2,1)S(1)} %collective-permute-done.26.refs_0_, bf16[80,4992]{1,0:T(8,128)(2,1)S(1)} %collective-permute-done.27.refs_1_, ...), custom_call_target="tpu_custom_call", output_to_operand_aliasing={{0}: (5, {}), {1}: (6, {})} | custom-call | flops 6000000 | bytes 1 | tf_op jit(solution)/shard_map/pallas_call | solution.py:228
  82.6 1.4 %collective-permute-start.32 = (bf16[2,80,4864]{2,1,0:T(8,128)(2,1)S(1)}, bf16[2,80,4864]{2,1,0:T(8,128)(2,1)S(1)}, u32[]{:S(2)}, u32[]{:S(2)}) collective-permute-start(bf16[2,80,4864]{2,1,0:T(8,128)(2,1)S(1)} %get-tuple-element.66), channel_id=1, source_target_pairs={{0,4},{4,0},{8,12},{12,8},{16,20},{20,16},{24,28},{28,24},{32,36},... | collective-permute-start | bytes 4669448 | tf_op jit(solution)/shard_map/ppermute | solution.py:51
  83.9 0.0 collective-permute-start.19
  83.9 5.4 %collective-permute-done.7.block.refs_1_ = bf16[80,4992]{1,0:T(8,128)(2,1)S(1)} collective-permute-done((bf16[80,4992]{1,0:T(8,128)(2,1)S(1)}, bf16[80,4992]{1,0:T(8,128)(2,1)S(1)}, u32[]{:S(2)}, u32[]{:S(2)}) %collective-permute-start.7) | collective-permute-done | bytes 798752 | tf_op jit(solution)/shard_map/ppermute | solution.py:51
  89.4 1.2 collective-permute-start.31
  90.6 5.8 %collective-permute-done.19.refs_0_ = bf16[80,4992]{1,0:T(8,128)(2,1)S(1)} collective-permute-done((bf16[80,4992]{1,0:T(8,128)(2,1)S(1)}, bf16[80,4992]{1,0:T(8,128)(2,1)S(1)}, u32[]{:S(2)}, u32[]{:S(2)}) %collective-permute-start.19) | collective-permute-done | bytes 798752 | tf_op jit(solution)/shard_map/ppermute | solution.py:51
  96.4 1.7 %shard_map.116 = (bf16[2560,2432]{1,0:T(8,128)(2,1)}, bf16[2560,2432]{1,0:T(8,128)(2,1)}, bf16[2,80,4864]{2,1,0:T(8,128)(2,1)S(1)}) custom-call(bf16[80,4992]{1,0:T(8,128)(2,1)S(1)} %collective-permute-done.19.refs_0_, bf16[80,4992]{1,0:T(8,128)(2,1)S(1)} %collective-permute-done.7.block.refs_1_, ...), custom_call_target="tpu_custom_call", output_to_operand_aliasing={{0}: (5, {}), {1}: (6, {})} | custom-call | flops 6000000 | bytes 1 | tf_op jit(solution)/shard_map/pallas_call | solution.py:228
  98.2 1.7 %collective-permute-start.29 = (bf16[2,80,4864]{2,1,0:T(8,128)(2,1)S(1)}, bf16[2,80,4864]{2,1,0:T(8,128)(2,1)S(1)}, u32[]{:S(2)}, u32[]{:S(2)}) collective-permute-start(bf16[2,80,4864]{2,1,0:T(8,128)(2,1)S(1)} %get-tuple-element.65), channel_id=1, source_target_pairs={{0,4},{4,0},{8,12},{12,8},{16,20},{20,16},{24,28},{28,24},{32,36},... | collective-permute-start | bytes 4669448 | tf_op jit(solution)/shard_map/ppermute | solution.py:51
  99.8 5.1 %collective-permute-done.30.refs_0_ = bf16[80,4992]{1,0:T(8,128)(2,1)S(1)} collective-permute-done((bf16[80,4992]{1,0:T(8,128)(2,1)S(1)}, bf16[80,4992]{1,0:T(8,128)(2,1)S(1)}, u32[]{:S(2)}, u32[]{:S(2)}) %collective-permute-start.30) | collective-permute-done | bytes 798752 | tf_op jit(solution)/shard_map/ppermute | solution.py:51
  105.0 1.7 %shard_map.117 = (bf16[2560,2432]{1,0:T(8,128)(2,1)}, bf16[2560,2432]{1,0:T(8,128)(2,1)}, bf16[2,80,4864]{2,1,0:T(8,128)(2,1)S(1)}) custom-call(bf16[80,4992]{1,0:T(8,128)(2,1)S(1)} %collective-permute-done.30.refs_0_, bf16[80,4992]{1,0:T(8,128)(2,1)S(1)} %collective-permute-done.31.refs_1_, ...), custom_call_target="tpu_custom_call", output_to_operand_aliasing={{0}: (5, {}), {1}: (6, {})} | custom-call | flops 6000000 | bytes 1 | tf_op jit(solution)/shard_map/pallas_call | solution.py:228
  106.7 1.7 %collective-permute-start.33 = (bf16[2,80,4864]{2,1,0:T(8,128)(2,1)S(1)}, bf16[2,80,4864]{2,1,0:T(8,128)(2,1)S(1)}, u32[]{:S(2)}, u32[]{:S(2)}) collective-permute-start(bf16[2,80,4864]{2,1,0:T(8,128)(2,1)S(1)} %get-tuple-element.69), channel_id=1, source_target_pairs={{0,4},{4,0},{8,12},{12,8},{16,20},{20,16},{24,28},{28,24},{32,36},... | collective-permute-start | bytes 4669448 | tf_op jit(solution)/shard_map/ppermute | solution.py:51
  108.4 0.1 shard_map.103
  108.4 0.1 collective-permute-start.17
  108.5 0.1 shard_map.106
  108.6 2.7 %collective-permute-start.18 = (bf16[48,4992]{1,0:T(8,128)(2,1)S(1)}, bf16[48,4992]{1,0:T(8,128)(2,1)S(1)}, u32[]{:S(2)}, u32[]{:S(2)}) collective-permute-start(bf16[48,4992]{1,0:T(8,128)(2,1)S(1)} %get-tuple-element.50), channel_id=1, source_target_pairs={{0,96},{4,28},{8,104},{12,4},{16,112},{20,12},{24,120},{28,20},{32... | collective-permute-start | bytes 1437704 | tf_op jit(solution)/shard_map/ppermute | solution.py:51
  111.3 6.3 %collective-permute-done.17.refs_0_ = bf16[48,4992]{1,0:T(8,128)(2,1)S(1)} collective-permute-done((bf16[48,4992]{1,0:T(8,128)(2,1)S(1)}, bf16[48,4992]{1,0:T(8,128)(2,1)S(1)}, u32[]{:S(2)}, u32[]{:S(2)}) %collective-permute-start.17) | collective-permute-done | bytes 479264 | tf_op jit(solution)/shard_map/ppermute | solution.py:51
  117.6 2.1 %shard_map.118 = (bf16[2560,2432]{1,0:T(8,128)(2,1)}, bf16[2560,2432]{1,0:T(8,128)(2,1)}, bf16[2,48,4864]{2,1,0:T(8,128)(2,1)S(1)}) custom-call(bf16[48,4992]{1,0:T(8,128)(2,1)S(1)} %collective-permute-done.17.refs_0_, bf16[48,4992]{1,0:T(8,128)(2,1)S(1)} %collective-permute-done.18.refs_1_, ...), custom_call_target="tpu_custom_call", output_to_operand_aliasing={{0}: (6, {}), {1}: (7, {})} | custom-call | flops 6000000 | bytes 1 | tf_op jit(solution)/shard_map/pallas_call | solution.py:228
  119.7 1.0 collective-permute-start.34
  120.6 2.7 %collective-permute-start.8 = (bf16[32,4992]{1,0:T(8,128)(2,1)S(1)}, bf16[32,4992]{1,0:T(8,128)(2,1)S(1)}, u32[]{:S(2)}, u32[]{:S(2)}) collective-permute-start(bf16[32,4992]{1,0:T(8,128)(2,1)S(1)} %get-tuple-element.46), channel_id=1, source_target_pairs={{0,96},{4,28},{8,104},{12,4},{16,112},{20,12},{24,120},{28,20},{32... | collective-permute-start | bytes 958472 | tf_op jit(solution)/shard_map/ppermute | solution.py:51
  123.3 4.7 %collective-permute-done.2.refs_0_ = bf16[32,4992]{1,0:T(8,128)(2,1)S(1)} collective-permute-done((bf16[32,4992]{1,0:T(8,128)(2,1)S(1)}, bf16[32,4992]{1,0:T(8,128)(2,1)S(1)}, u32[]{:S(2)}, u32[]{:S(2)}) %collective-permute-start.2) | collective-permute-done | bytes 319520 | tf_op jit(solution)/shard_map/ppermute | solution.py:51
  128.0 1.1 collective-permute-start.3
  129.0 0.0 collective-permute-start.9
  129.0 0.6 slice_reduce_fusion
  129.7 1.1 shard_map.119
  130.8 1.4 %shard_map.120 = (bf16[2560,2432]{1,0:T(8,128)(2,1)}, bf16[2560,2432]{1,0:T(8,128)(2,1)}) custom-call(bf16[32,4992]{1,0:T(8,128)(2,1)S(1)} %collective-permute-done.3.refs_0_, bf16[32,4992]{1,0:T(8,128)(2,1)S(1)} %collective-permute-done.9.refs_1_, ...), custom_call_target="tpu_custom_call", output_to_operand_aliasing={{0}: (5, {}), {1}: (6, {})} | custom-call | flops 6000000 | bytes 1 | tf_op jit(solution)/shard_map/pallas_call | solution.py:228
  (26 shorter events, 0.1 us)
Async XLA Ops:
  1.9 21.9 %collective-permute-start = (bf16[80,4992]{1,0:T(8,128)(2,1)S(1)}, bf16[80,4992]{1,0:T(8,128)(2,1)S(1)}, u32[]{:S(2)}, u32[]{:S(2)}) collective-permute-start(bf16[80,4992]{1,0:T(8,128)(2,1)S(1)} %get-tuple-element.42.block.refs_0_), channel_id=1, source_target_pairs={{0,8},{4,36},{8,16},{12,44},{16,24},{20,52},{24,0},{28,60},{32,40}... | collective-permute-start | bytes 2396168 | tf_op jit(solution)/shard_map/ppermute | solution.py:51
  4.6 4.4 %collective-permute-start.10 = (f32[1,4864]{1,0:T(1,128)S(1)}, f32[1,4864]{1,0:T(1,128)S(1)}, u32[]{:S(2)}, u32[]{:S(2)}) collective-permute-start(f32[1,4864]{1,0:T(1,128)S(1)} %shard_map.107.own), channel_id=1, source_target_pairs={{0,32},{4,12},{8,40},{12,20},{16,48},{20,28},{24,56},{28,4},{32,64... | collective-permute-start | bytes 58376 | tf_op jit(solution)/shard_map/ppermute | solution.py:51
  5.9 3.1 %collective-permute-start.11 = (f32[1,4864]{1,0:T(1,128)S(1)}, f32[1,4864]{1,0:T(1,128)S(1)}, u32[]{:S(2)}, u32[]{:S(2)}) collective-permute-start(f32[1,4864]{1,0:T(1,128)S(1)} %shard_map.107.own), channel_id=1, source_target_pairs={{0,96},{4,28},{8,104},{12,4},{16,112},{20,12},{24,120},{28,20},{32... | collective-permute-start | bytes 58376 | tf_op jit(solution)/shard_map/ppermute | solution.py:51
  7.3 4.3 %collective-permute-start.12 = (f32[1,4864]{1,0:T(1,128)S(1)}, f32[1,4864]{1,0:T(1,128)S(1)}, u32[]{:S(2)}, u32[]{:S(2)}) collective-permute-start(f32[1,4864]{1,0:T(1,128)S(1)} %shard_map.107.own), channel_id=1, source_target_pairs={{0,64},{4,20},{8,72},{12,28},{16,80},{20,4},{24,88},{28,12},{32,96... | collective-permute-start | bytes 58376 | tf_op jit(solution)/shard_map/ppermute | solution.py:51
  11.7 4.3 %collective-permute-start.13 = (f32[1,4864]{1,0:T(1,128)S(1)}, f32[1,4864]{1,0:T(1,128)S(1)}, u32[]{:S(2)}, u32[]{:S(2)}) collective-permute-start(f32[1,4864]{1,0:T(1,128)S(1)} %shard_map.108.own), channel_id=1, source_target_pairs={{0,8},{4,36},{8,16},{12,44},{16,24},{20,52},{24,0},{28,60},{32,40}... | collective-permute-start | bytes 58376 | tf_op jit(solution)/shard_map/ppermute | solution.py:51
  13.0 3.0 %collective-permute-start.14 = (f32[1,4864]{1,0:T(1,128)S(1)}, f32[1,4864]{1,0:T(1,128)S(1)}, u32[]{:S(2)}, u32[]{:S(2)}) collective-permute-start(f32[1,4864]{1,0:T(1,128)S(1)} %shard_map.108.own), channel_id=1, source_target_pairs={{0,24},{4,100},{8,0},{12,108},{16,8},{20,116},{24,16},{28,124},{32... | collective-permute-start | bytes 58376 | tf_op jit(solution)/shard_map/ppermute | solution.py:51
  14.4 4.1 %collective-permute-start.15 = (f32[1,4864]{1,0:T(1,128)S(1)}, f32[1,4864]{1,0:T(1,128)S(1)}, u32[]{:S(2)}, u32[]{:S(2)}) collective-permute-start(f32[1,4864]{1,0:T(1,128)S(1)} %shard_map.108.own), channel_id=1, source_target_pairs={{0,16},{4,68},{8,24},{12,76},{16,0},{20,84},{24,8},{28,92},{32,48}... | collective-permute-start | bytes 58376 | tf_op jit(solution)/shard_map/ppermute | solution.py:51
  18.6 5.2 %collective-permute-start.16 = (f32[1,4864]{1,0:T(1,128)S(1)}, f32[1,4864]{1,0:T(1,128)S(1)}, u32[]{:S(2)}, u32[]{:S(2)}) collective-permute-start(f32[1,4864]{1,0:T(1,128)S(1)} %shard_map.109.mine), channel_id=1, source_target_pairs={{0,4},{4,0},{8,12},{12,8},{16,20},{20,16},{24,28},{28,24},{32,36},... | collective-permute-start | bytes 58376 | tf_op jit(solution)/shard_map/ppermute | solution.py:51
  25.4 27.4 %collective-permute-start.24 = (bf16[2,80,4864]{2,1,0:T(8,128)(2,1)S(1)}, bf16[2,80,4864]{2,1,0:T(8,128)(2,1)S(1)}, u32[]{:S(2)}, u32[]{:S(2)}) collective-permute-start(bf16[2,80,4864]{2,1,0:T(8,128)(2,1)S(1)} %get-tuple-element.54), channel_id=1, source_target_pairs={{0,4},{4,0},{8,12},{12,8},{16,20},{20,16},{24,28},{28,24},{32,36},... | collective-permute-start | bytes 4669448 | tf_op jit(solution)/shard_map/ppermute | solution.py:51
  25.8 18.5 %collective-permute-start.4 = (bf16[80,4992]{1,0:T(8,128)(2,1)S(1)}, bf16[80,4992]{1,0:T(8,128)(2,1)S(1)}, u32[]{:S(2)}, u32[]{:S(2)}) collective-permute-start(bf16[80,4992]{1,0:T(8,128)(2,1)S(1)} %get-tuple-element.42.block.refs_0_), channel_id=1, source_target_pairs={{0,24},{4,100},{8,0},{12,108},{16,8},{20,116},{24,16},{28,124},{32... | collective-permute-start | bytes 2396168 | tf_op jit(solution)/shard_map/ppermute | solution.py:51
  27.1 20.0 %collective-permute-start.21 = (bf16[80,4992]{1,0:T(8,128)(2,1)S(1)}, bf16[80,4992]{1,0:T(8,128)(2,1)S(1)}, u32[]{:S(2)}, u32[]{:S(2)}) collective-permute-start(bf16[80,4992]{1,0:T(8,128)(2,1)S(1)} %get-tuple-element.42.block.refs_0_), channel_id=1, source_target_pairs={{0,32},{4,12},{8,40},{12,20},{16,48},{20,28},{24,56},{28,4},{32,64... | collective-permute-start | bytes 2396168 | tf_op jit(solution)/shard_map/ppermute | solution.py:51
  27.2 20.0 %collective-permute-start.22 = (bf16[80,4992]{1,0:T(8,128)(2,1)S(1)}, bf16[80,4992]{1,0:T(8,128)(2,1)S(1)}, u32[]{:S(2)}, u32[]{:S(2)}) collective-permute-start(bf16[80,4992]{1,0:T(8,128)(2,1)S(1)} %get-tuple-element.42.block.refs_0_), channel_id=1, source_target_pairs={{0,96},{4,28},{8,104},{12,4},{16,112},{20,12},{24,120},{28,20},{32... | collective-permute-start | bytes 2396168 | tf_op jit(solution)/shard_map/ppermute | solution.py:51
  44.4 8.4 %collective-permute-start.5 = (bf16[80,2560]{1,0:T(8,128)(2,1)S(1)}, bf16[80,2560]{1,0:T(8,128)(2,1)S(1)}, u32[]{:S(2)}, u32[]{:S(2)}) collective-permute-start(bf16[80,2560]{1,0:T(8,128)(2,1)S(1)} %get-tuple-element.44), channel_id=1, source_target_pairs={{0,8},{4,36},{8,16},{12,44},{16,24},{20,52},{24,0},{28,60},{32,40}... | collective-permute-start | bytes 1228808 | tf_op jit(solution)/shard_map/ppermute | solution.py:51
  44.5 7.3 %collective-permute-start.6 = (bf16[80,2432]{1,0:T(8,128)(2,1)S(1)}, bf16[80,2432]{1,0:T(8,128)(2,1)S(1)}, u32[]{:S(2)}, u32[]{:S(2)}) collective-permute-start(bf16[80,2432]{1,0:T(8,128)(2,1)S(1)} %get-tuple-element.45), channel_id=1, source_target_pairs={{0,24},{4,100},{8,0},{12,108},{16,8},{20,116},{24,16},{28,124},{32... | collective-permute-start | bytes 1167368 | tf_op jit(solution)/shard_map/ppermute | solution.py:51
  47.1 16.0 %collective-permute-start.1 = (bf16[80,4992]{1,0:T(8,128)(2,1)S(1)}, bf16[80,4992]{1,0:T(8,128)(2,1)S(1)}, u32[]{:S(2)}, u32[]{:S(2)}) collective-permute-start(bf16[80,4992]{1,0:T(8,128)(2,1)S(1)} %collective-permute-done.a.refs_1_), channel_id=1, source_target_pairs={{0,32},{4,12},{8,40},{12,20},{16,48},{20,28},{24,56},{28,4},{32,64... | collective-permute-start | bytes 2396168 | tf_op jit(solution)/shard_map/ppermute | solution.py:51
  48.8 24.7 %collective-permute-start.23 = (bf16[2,80,4864]{2,1,0:T(8,128)(2,1)S(1)}, bf16[2,80,4864]{2,1,0:T(8,128)(2,1)S(1)}, u32[]{:S(2)}, u32[]{:S(2)}) collective-permute-start(bf16[2,80,4864]{2,1,0:T(8,128)(2,1)S(1)} %get-tuple-element.53), channel_id=1, source_target_pairs={{0,4},{4,0},{8,12},{12,8},{16,20},{20,16},{24,28},{28,24},{32,36},... | collective-permute-start | bytes 4669448 | tf_op jit(solution)/shard_map/ppermute | solution.py:51
  54.6 26.2 %collective-permute-start.28 = (bf16[2,80,4864]{2,1,0:T(8,128)(2,1)S(1)}, bf16[2,80,4864]{2,1,0:T(8,128)(2,1)S(1)}, u32[]{:S(2)}, u32[]{:S(2)}) collective-permute-start(bf16[2,80,4864]{2,1,0:T(8,128)(2,1)S(1)} %get-tuple-element.60), channel_id=1, source_target_pairs={{0,4},{4,0},{8,12},{12,8},{16,20},{20,16},{24,28},{28,24},{32,36},... | collective-permute-start | bytes 4669448 | tf_op jit(solution)/shard_map/ppermute | solution.py:51
  61.0 11.3 %collective-permute-start.20 = (bf16[80,4992]{1,0:T(8,128)(2,1)S(1)}, bf16[80,4992]{1,0:T(8,128)(2,1)S(1)}, u32[]{:S(2)}, u32[]{:S(2)}) collective-permute-start(bf16[80,4992]{1,0:T(8,128)(2,1)S(1)} %collective-permute-done.4.b.refs_0_), channel_id=1, source_target_pairs={{0,96},{4,28},{8,104},{12,4},{16,112},{20,12},{24,120},{28,20},{32... | collective-permute-start | bytes 2396168 | tf_op jit(solution)/shard_map/ppermute | solution.py:51
  61.0 18.1 %collective-permute-start.26 = (bf16[80,4992]{1,0:T(8,128)(2,1)S(1)}, bf16[80,4992]{1,0:T(8,128)(2,1)S(1)}, u32[]{:S(2)}, u32[]{:S(2)}) collective-permute-start(bf16[80,4992]{1,0:T(8,128)(2,1)S(1)} %collective-permute-done.4.b.refs_0_), channel_id=1, source_target_pairs={{0,32},{4,12},{8,40},{12,20},{16,48},{20,28},{24,56},{28,4},{32,64... | collective-permute-start | bytes 2396168 | tf_op jit(solution)/shard_map/ppermute | solution.py:51
  63.1 17.7 %collective-permute-start.27 = (bf16[80,4992]{1,0:T(8,128)(2,1)S(1)}, bf16[80,4992]{1,0:T(8,128)(2,1)S(1)}, u32[]{:S(2)}, u32[]{:S(2)}) collective-permute-start(bf16[80,4992]{1,0:T(8,128)(2,1)S(1)} %collective-permute-done.a.refs_1_), channel_id=1, source_target_pairs={{0,96},{4,28},{8,104},{12,4},{16,112},{20,12},{24,120},{28,20},{32... | collective-permute-start | bytes 2396168 | tf_op jit(solution)/shard_map/ppermute | solution.py:51
  72.2 17.1 %collective-permute-start.7 = (bf16[80,4992]{1,0:T(8,128)(2,1)S(1)}, bf16[80,4992]{1,0:T(8,128)(2,1)S(1)}, u32[]{:S(2)}, u32[]{:S(2)}) collective-permute-start(bf16[80,4992]{1,0:T(8,128)(2,1)S(1)} %shard_map.105.refs_1_), channel_id=1, source_target_pairs={{0,96},{4,28},{8,104},{12,4},{16,112},{20,12},{24,120},{28,20},{32... | collective-permute-start | bytes 2396168 | tf_op jit(solution)/shard_map/ppermute | solution.py:51
  75.2 21.2 %collective-permute-start.25 = (bf16[2,80,4864]{2,1,0:T(8,128)(2,1)S(1)}, bf16[2,80,4864]{2,1,0:T(8,128)(2,1)S(1)}, u32[]{:S(2)}, u32[]{:S(2)}) collective-permute-start(bf16[2,80,4864]{2,1,0:T(8,128)(2,1)S(1)} %get-tuple-element.59), channel_id=1, source_target_pairs={{0,4},{4,0},{8,12},{12,8},{16,20},{20,16},{24,28},{28,24},{32,36},... | collective-permute-start | bytes 4669448 | tf_op jit(solution)/shard_map/ppermute | solution.py:51
  82.6 22.4 %collective-permute-start.32 = (bf16[2,80,4864]{2,1,0:T(8,128)(2,1)S(1)}, bf16[2,80,4864]{2,1,0:T(8,128)(2,1)S(1)}, u32[]{:S(2)}, u32[]{:S(2)}) collective-permute-start(bf16[2,80,4864]{2,1,0:T(8,128)(2,1)S(1)} %get-tuple-element.66), channel_id=1, source_target_pairs={{0,4},{4,0},{8,12},{12,8},{16,20},{20,16},{24,28},{28,24},{32,36},... | collective-permute-start | bytes 4669448 | tf_op jit(solution)/shard_map/ppermute | solution.py:51
  83.9 12.5 %collective-permute-start.19 = (bf16[80,4992]{1,0:T(8,128)(2,1)S(1)}, bf16[80,4992]{1,0:T(8,128)(2,1)S(1)}, u32[]{:S(2)}, u32[]{:S(2)}) collective-permute-start(bf16[80,4992]{1,0:T(8,128)(2,1)S(1)} %shard_map.105.refs_1_), channel_id=1, source_target_pairs={{0,32},{4,12},{8,40},{12,20},{16,48},{20,28},{24,56},{28,4},{32,64... | collective-permute-start | bytes 2396168 | tf_op jit(solution)/shard_map/ppermute | solution.py:51
  83.9 21.0 %collective-permute-start.30 = (bf16[80,4992]{1,0:T(8,128)(2,1)S(1)}, bf16[80,4992]{1,0:T(8,128)(2,1)S(1)}, u32[]{:S(2)}, u32[]{:S(2)}) collective-permute-start(bf16[80,4992]{1,0:T(8,128)(2,1)S(1)} %collective-permute-done.21.refs_0_), channel_id=1, source_target_pairs={{0,32},{4,12},{8,40},{12,20},{16,48},{20,28},{24,56},{28,4},{32,64... | collective-permute-start | bytes 2396168 | tf_op jit(solution)/shard_map/ppermute | solution.py:51
  89.4 15.6 %collective-permute-start.31 = (bf16[80,4992]{1,0:T(8,128)(2,1)S(1)}, bf16[80,4992]{1,0:T(8,128)(2,1)S(1)}, u32[]{:S(2)}, u32[]{:S(2)}) collective-permute-start(bf16[80,4992]{1,0:T(8,128)(2,1)S(1)} %collective-permute-done.20.refs_1_), channel_id=1, source_target_pairs={{0,96},{4,28},{8,104},{12,4},{16,112},{20,12},{24,120},{28,20},{32... | collective-permute-start | bytes 2396168 | tf_op jit(solution)/shard_map/ppermute | solution.py:51
  98.2 19.4 %collective-permute-start.29 = (bf16[2,80,4864]{2,1,0:T(8,128)(2,1)S(1)}, bf16[2,80,4864]{2,1,0:T(8,128)(2,1)S(1)}, u32[]{:S(2)}, u32[]{:S(2)}) collective-permute-start(bf16[2,80,4864]{2,1,0:T(8,128)(2,1)S(1)} %get-tuple-element.65), channel_id=1, source_target_pairs={{0,4},{4,0},{8,12},{12,8},{16,20},{20,16},{24,28},{28,24},{32,36},... | collective-permute-start | bytes 4669448 | tf_op jit(solution)/shard_map/ppermute | solution.py:51
  106.7 10.8 %collective-permute-start.33 = (bf16[2,80,4864]{2,1,0:T(8,128)(2,1)S(1)}, bf16[2,80,4864]{2,1,0:T(8,128)(2,1)S(1)}, u32[]{:S(2)}, u32[]{:S(2)}) collective-permute-start(bf16[2,80,4864]{2,1,0:T(8,128)(2,1)S(1)} %get-tuple-element.69), channel_id=1, source_target_pairs={{0,4},{4,0},{8,12},{12,8},{16,20},{20,16},{24,28},{28,24},{32,36},... | collective-permute-start | bytes 4669448 | tf_op jit(solution)/shard_map/ppermute | solution.py:51
  108.4 9.1 %collective-permute-start.17 = (bf16[48,4992]{1,0:T(8,128)(2,1)S(1)}, bf16[48,4992]{1,0:T(8,128)(2,1)S(1)}, u32[]{:S(2)}, u32[]{:S(2)}) collective-permute-start(bf16[48,4992]{1,0:T(8,128)(2,1)S(1)} %get-tuple-element.49), channel_id=1, source_target_pairs={{0,32},{4,12},{8,40},{12,20},{16,48},{20,28},{24,56},{28,4},{32,64... | collective-permute-start | bytes 1437704 | tf_op jit(solution)/shard_map/ppermute | solution.py:51
  108.6 9.0 %collective-permute-start.18 = (bf16[48,4992]{1,0:T(8,128)(2,1)S(1)}, bf16[48,4992]{1,0:T(8,128)(2,1)S(1)}, u32[]{:S(2)}, u32[]{:S(2)}) collective-permute-start(bf16[48,4992]{1,0:T(8,128)(2,1)S(1)} %get-tuple-element.50), channel_id=1, source_target_pairs={{0,96},{4,28},{8,104},{12,4},{16,112},{20,12},{24,120},{28,20},{32... | collective-permute-start | bytes 1437704 | tf_op jit(solution)/shard_map/ppermute | solution.py:51
  119.7 11.2 %collective-permute-start.34 = (bf16[2,48,4864]{2,1,0:T(8,128)(2,1)S(1)}, bf16[2,48,4864]{2,1,0:T(8,128)(2,1)S(1)}, u32[]{:S(2)}, u32[]{:S(2)}) collective-permute-start(bf16[2,48,4864]{2,1,0:T(8,128)(2,1)S(1)} %get-tuple-element.72), channel_id=1, source_target_pairs={{0,4},{4,0},{8,12},{12,8},{16,20},{20,16},{24,28},{28,24},{32,36},... | collective-permute-start | bytes 2801672 | tf_op jit(solution)/shard_map/ppermute | solution.py:51
  120.6 7.3 %collective-permute-start.2 = (bf16[32,4992]{1,0:T(8,128)(2,1)S(1)}, bf16[32,4992]{1,0:T(8,128)(2,1)S(1)}, u32[]{:S(2)}, u32[]{:S(2)}) collective-permute-start(bf16[32,4992]{1,0:T(8,128)(2,1)S(1)} %get-tuple-element.43), channel_id=1, source_target_pairs={{0,32},{4,12},{8,40},{12,20},{16,48},{20,28},{24,56},{28,4},{32,64... | collective-permute-start | bytes 958472 | tf_op jit(solution)/shard_map/ppermute | solution.py:51
  120.6 8.4 %collective-permute-start.8 = (bf16[32,4992]{1,0:T(8,128)(2,1)S(1)}, bf16[32,4992]{1,0:T(8,128)(2,1)S(1)}, u32[]{:S(2)}, u32[]{:S(2)}) collective-permute-start(bf16[32,4992]{1,0:T(8,128)(2,1)S(1)} %get-tuple-element.46), channel_id=1, source_target_pairs={{0,96},{4,28},{8,104},{12,4},{16,112},{20,12},{24,120},{28,20},{32... | collective-permute-start | bytes 958472 | tf_op jit(solution)/shard_map/ppermute | solution.py:51
  128.0 2.8 %collective-permute-start.3 = (bf16[32,4992]{1,0:T(8,128)(2,1)S(1)}, bf16[32,4992]{1,0:T(8,128)(2,1)S(1)}, u32[]{:S(2)}, u32[]{:S(2)}) collective-permute-start(bf16[32,4992]{1,0:T(8,128)(2,1)S(1)} %collective-permute-done.2.refs_0_), channel_id=1, source_target_pairs={{0,4},{4,0},{8,12},{12,8},{16,20},{20,16},{24,28},{28,24},{32,36},... | collective-permute-start | bytes 958472 | tf_op jit(solution)/shard_map/ppermute | solution.py:51
  129.0 1.8 %collective-permute-start.9 = (bf16[32,4992]{1,0:T(8,128)(2,1)S(1)}, bf16[32,4992]{1,0:T(8,128)(2,1)S(1)}, u32[]{:S(2)}, u32[]{:S(2)}) collective-permute-start(bf16[32,4992]{1,0:T(8,128)(2,1)S(1)} %collective-permute-done.8.refs_1_), channel_id=1, source_target_pairs={{0,4},{4,0},{8,12},{12,8},{16,20},{20,16},{24,28},{28,24},{32,36},... | collective-permute-start | bytes 958472 | tf_op jit(solution)/shard_map/ppermute | solution.py:51
